TPU v7x, 128 devices: a whole 4x4x4 slice. The times are simulated.
128 devices in a mesh: ctx: 32 (over x, z_lo, y), tp: 4 (over z_hi, core).
Axes of the slice: x: 4, y: 4, z: 4 (z_hi: 2, z_lo: 2; z = z_hi * 2 + z_lo), core: 2. Of those that a mesh axis runs over, the one named last changes fastest.
Arguments:
- resid: bfloat16 [65536, 4096], P('ctx', 'tp'), may hold values from -6 to 6
- sel_blocks: int32 [64], P('ctx'), may hold values from 0 to 511, as said below
- norm_gain: float32 [4096], replicated, may hold values from 0.5 to 1.5
- router_weight: float32 [4096], replicated, may hold values from -0.09375 to 0.09375
- w_query: bfloat16 [4096, 4096], P(None, 'tp'), may hold values from -0.25 to 0.25
- w_key: bfloat16 [4096, 512], P(None, 'tp'), may hold values from -4 to 4
- value_projection: bfloat16 [4096, 512], P(None, 'tp'), may hold values from -0.09375 to 0.09375
- w_out: bfloat16 [4096, 4096], P('tp'), may hold values from -0.09375 to 0.09375
Outputs:
- mixed: bfloat16 [8192, 4096], P(('ctx', 'tp'))
Inputs may be any that keep to these rules, and one draw needn't show every extreme that they name: `sel_blocks`: entries 2 * c to 2 * c + 1 are 2 different numbers from c * 16 to c * 16 + 15, increasing.
All inputs are finite; a program needn't handle non-finite values.
Results may differ from a plain program's by a relative error of at most 0.0075.
Values may be sent and summed in bfloat16 or wider, within the bound.
A program may use at most 128 MiB of HBM per device.

v0:
```python
import math

import jax
import jax.numpy as jnp
from jax import lax
from jax.sharding import PartitionSpec as P

HEAD_WIDTH = 128
BLK = 128


rope_base = 500000.0
norm_eps = 1e-05
masked_score = -1e30


def joined_along(parts, dim):
    dims = list(parts.shape[1:])
    dims[dim] *= parts.shape[0]
    return jnp.moveaxis(parts, 0, dim).reshape(dims)


def sent_to_all(value, axis):
    devices = lax.axis_size(axis)
    return lax.all_to_all(
        jnp.broadcast_to(value[None], (devices, *value.shape)), axis, 0, 0, tiled=True
    )


def gathered_copies(value, axis, dim):
    return joined_along(sent_to_all(value, axis), dim)


def sent_together(arrays, axis, dim, along):
    widths = [a.shape[along] for a in arrays]
    both = jnp.concatenate(arrays, axis=along)
    result = lax.all_gather(both, axis, axis=dim, tiled=True)
    return tuple(jnp.split(result, [sum(widths[:k]) for k in range(1, len(widths))], axis=along))


def in_blocks(value, dim, devices):
    dims = value.shape
    parts = value.reshape(*dims[:dim], devices, dims[dim] // devices, *dims[dim + 1 :])
    return jnp.moveaxis(parts, dim, 0)


def sent_and_summed(value, axis, dim):
    parts = in_blocks(value, dim, lax.axis_size(axis))
    arrived = lax.all_to_all(parts, axis, split_axis=0, concat_axis=0, tiled=True)
    return arrived.astype(jnp.float32).sum(axis=0)


def rotate_heads(values_in, positions, head_size):
    rows = values_in.shape[0]
    heads = values_in.shape[1] // head_size
    shaped = values_in.reshape(rows, heads, head_size)
    half_size = head_size // 2
    freqs = jnp.exp(
        jnp.arange(half_size, dtype=jnp.float32) * (-2.0 * math.log(rope_base) / head_size)
    )
    angles = positions.astype(jnp.float32)[:, None] * freqs[None, :]
    cosine = jnp.cos(angles)[:, None, :]
    sine = jnp.sin(angles)[:, None, :]
    first = shaped[:, :, :half_size]
    second = shaped[:, :, half_size:]
    turned = jnp.concatenate(
        [first * cosine - second * sine, second * cosine + first * sine], axis=2
    )
    return turned.reshape(rows, heads * head_size).astype(jnp.bfloat16)


def on_device(resid, sel_blocks, norm_gain, router_weight, w_query, w_key, value_projection, w_out):
    picked_blocks = sel_blocks.shape[0]
    local_rows, local_width = resid.shape
    block_count = local_rows // BLK
    local_ids = sel_blocks - lax.axis_index("ctx") * block_count
    onehot = (local_ids[:, None] == jnp.arange(block_count, dtype=jnp.int32)[None, :]).astype(
        jnp.bfloat16
    )
    flat_blocks = resid.reshape(block_count, BLK * local_width)
    picked = jnp.dot(onehot, flat_blocks, preferred_element_type=jnp.float32).astype(jnp.bfloat16)
    picked = picked.reshape(picked_blocks * BLK, local_width)
    chosen = gathered_copies(picked, "tp", 1)
    sel_rows = chosen.shape[0]
    positions = (sel_blocks[:, None] * BLK + jnp.arange(BLK, dtype=jnp.int32)[None, :]).reshape(
        sel_rows
    )
    chosen_wide = chosen.astype(jnp.float32)
    inv_rms = lax.rsqrt(jnp.mean(chosen_wide * chosen_wide, axis=1) + norm_eps)
    normed = (chosen_wide * inv_rms[:, None] * norm_gain[None, :]).astype(jnp.bfloat16)
    gate = jax.nn.sigmoid(jnp.sum(chosen_wide * router_weight[None, :], axis=1))
    queries = rotate_heads(
        jnp.dot(normed, w_query, preferred_element_type=jnp.float32), positions, HEAD_WIDTH
    )
    key_matrix = rotate_heads(
        jnp.dot(normed, w_key, preferred_element_type=jnp.float32), positions, HEAD_WIDTH
    )
    values = jnp.dot(normed, value_projection, preferred_element_type=jnp.float32).astype(
        jnp.bfloat16
    )
    kv_heads = w_key.shape[1] // HEAD_WIDTH
    q_heads = w_query.shape[1] // HEAD_WIDTH
    group = q_heads // kv_heads
    score_scale = 1.0 / math.sqrt(HEAD_WIDTH)

    def fresh_state(rows):
        return (
            jnp.full((kv_heads, group * rows), masked_score, jnp.float32),
            jnp.zeros((kv_heads, group * rows), jnp.float32),
            jnp.zeros((kv_heads, group * rows, HEAD_WIDTH), jnp.float32),
        )

    def fold_block(state, query_set, key_block, value_block, key_pos):
        query_group, query_pos = query_set
        highest, total, accum = state
        rows = key_block.shape[0]
        per_head_keys = key_block.reshape(rows, kv_heads, HEAD_WIDTH)
        per_head_values = value_block.reshape(rows, kv_heads, HEAD_WIDTH)
        scores = (
            jnp.einsum(
                "hqe,khe->hqk", query_group, per_head_keys, preferred_element_type=jnp.float32
            )
            * score_scale
        )
        allowed = key_pos[None, None, :] <= query_pos[None, :, None]
        scores = jnp.where(allowed, scores, masked_score)
        new_high = jnp.maximum(highest, jnp.max(scores, axis=2))
        shrink = jnp.exp(highest - new_high)
        expd = jnp.where(allowed, jnp.exp(scores - new_high[:, :, None]), 0.0)
        total = total * shrink + jnp.sum(expd, axis=2)
        accum = accum * shrink[:, :, None] + jnp.einsum(
            "hqk,khe->hqe",
            expd.astype(jnp.bfloat16),
            per_head_values,
            preferred_element_type=jnp.float32,
        )
        return (new_high, total, accum)

    def guarded(state, query_set, key_block, value_block, key_pos):
        needed = jnp.min(key_pos) <= jnp.max(query_set[1])
        return lax.cond(
            needed,
            lambda current: fold_block(current, query_set, key_block, value_block, key_pos),
            lambda current: current,
            state,
        )

    group_rows = queries.shape[0]
    grouped = (
        queries.reshape(group_rows, kv_heads, group, HEAD_WIDTH)
        .transpose(1, 2, 0, 3)
        .reshape(kv_heads, group * group_rows, HEAD_WIDTH)
    )
    query_sets = ((grouped, jnp.tile(positions, group)),)
    set_rows = (sel_rows,)
    init_states = tuple((fresh_state(rows) for rows in set_rows))
    key_rows, value_rows, key_pos = (
        *sent_together((key_matrix, values), "ctx", 0, 1),
        lax.all_gather(positions, "ctx", axis=0, tiled=True),
    )
    rows = key_rows.shape[0]
    block_rows = rows
    while block_rows > 1024 and block_rows % 2 == 0:
        block_rows = block_rows // 2
    block_total = rows // block_rows
    stacked = (
        key_rows.reshape(block_total, block_rows, key_rows.shape[1]),
        value_rows.reshape(block_total, block_rows, value_rows.shape[1]),
        key_pos.reshape(block_total, block_rows),
    )

    def step_block(current, blocks):
        updated = tuple(
            (
                guarded(current[index], query_sets[index], blocks[0], blocks[1], blocks[2])
                for index in range(len(query_sets))
            )
        )
        return (updated, None)

    result, unused = lax.scan(step_block, init_states, stacked)
    state = result[0]
    merged = state[2] / state[1][:, :, None]
    merged = merged.reshape(kv_heads, group, sel_rows, HEAD_WIDTH).transpose(2, 0, 1, 3)
    attended = merged.reshape(sel_rows, q_heads * HEAD_WIDTH).astype(jnp.bfloat16)
    share_rows = sel_rows // lax.axis_size("tp")
    projected = sent_and_summed(
        jnp.dot(attended, w_out, preferred_element_type=jnp.float32).astype(jnp.bfloat16), "tp", 0
    )
    first_row = lax.axis_index("tp") * share_rows
    own_chosen = lax.dynamic_slice_in_dim(chosen_wide, first_row, share_rows, 0)
    own_gate = lax.dynamic_slice_in_dim(gate, first_row, share_rows, 0)
    return (own_chosen + own_gate[:, None] * projected).astype(jnp.bfloat16)


def solution(mesh):
    return jax.shard_map(
        on_device,
        mesh=mesh,
        in_specs=(
            P("ctx", "tp"),
            P("ctx"),
            P(),
            P(),
            P(None, "tp"),
            P(None, "tp"),
            P(None, "tp"),
            P("tp", None),
        ),
        out_specs=P(("ctx", "tp"), None),
        check_vma=False,
    )
```

profile of v0, /device:TPU:46, one launch (start us, length us, event | category | flops | bytes accessed | tf_op | source)
XLA Modules:
  0.0 342.2 jit_solution(14965188761115279166)
XLA Ops:
  6.5 4.9 %reshape.261 = bf16[16,131072]{1,0:T(8,128)(2,1)} reshape(bf16[2048,1024]{1,0:T(8,128)(2,1)} %param.12) | data formatting | bytes 8388608 | tf_op jit(solution)/shard_map/reshape | solution.py:80
  11.5 3.0 convolution_convert_fusion
  15.0 1.6 broadcast_in_dim.17
  16.5 4.4 %all-to-all-start = ((bf16[4,256,1024]{2,1,0:T(8,128)(2,1)}), bf16[4,256,1024]{2,1,0:T(8,128)(2,1)}, u32[]{:S(2)}, u32[]{:S(2)}) async-start(bf16[4,256,1024]{2,1,0:T(8,128)(2,1)} %broadcast_in_dim.17), calls=%async_computation | async-start | bytes 4194304 | tf_op jit(solution)/shard_map/all_to_all | solution.py:25
  21.2 27.1 %all-to-all-done = bf16[4,256,1024]{2,1,0:T(8,128)(2,1)} async-done(((bf16[4,256,1024]{2,1,0:T(8,128)(2,1)}), bf16[4,256,1024]{2,1,0:T(8,128)(2,1)}, u32[]{:S(2)}, u32[]{:S(2)}) %all-to-all-start) | async-done | bytes 2097184 | tf_op jit(solution)/shard_map/all_to_all | solution.py:25
  48.2 2.8 copy.42
  51.1 0.8 multiply_reduce_fusion.1
  51.9 0.7 multiply_convert_fusion.1
  54.1 0.7 pad_maximum_fusion
  54.8 11.2 %copy.53 = bf16[1024,4096]{1,0:T(8,128)(2,1)} copy(bf16[1024,4096]{0,1:T(8,128)(2,1)} %bitcast.85) | data formatting | bytes 16777216 | tf_op jit(solution)/shard_map/dot_general | solution.py:93
  66.1 71.9 %all-gather = s32[32,1,256]{2,1,0:T(1,128)S(1)} all-gather(s32[1,1,256]{2,1,0:T(1,128)S(1)} %bitcast.105), channel_id=1, replica_groups=mesh['ctx'=32,'tp'=4] {'ctx'}, dimensions={0}, use_global_device_ids=true | all-gather | bytes 33792 | tf_op jit(solution)/shard_map/all_gather | solution.py:159
  138.1 0.6 broadcast_reduce_fusion
  139.0 0.7 multiply_convert_fusion
  139.8 5.7 %fusion.40 = f32[256,8,128]{0,2,1:T(8,128)S(1)} fusion(bf16[256,4096,1]{0,1,2:T(8,128)(2,1)S(1)} %bitcast.90, bf16[8,128,4096]{2,1,0:T(8,128)(2,1)} %bitcast.86), kind=kOutput, calls=%fused_computation.69 | convolution fusion | flops 2147483648 | bytes 11534336 | tf_op jit(solution)/shard_map/dot_general | solution.py:93
  145.7 1.0 copy.46
  146.7 43.7 %all-gather.3.cloned.1.call-done = bf16[8192,256]{0,1:T(8,128)(2,1)} async-done(((bf16[256,256]{0,1:T(8,128)(2,1)}), bf16[8192,256]{0,1:T(8,128)(2,1)}) %all-gather.3.cloned.1.call-update) | async-done | bytes 4194320 | tf_op jit(solution)/shard_map/all_gather | solution.py:37
  190.4 4.6 %fusion.39 = (bf16[8192,128]{0,1:T(8,128)(2,1)}, bf16[8192,128]{0,1:T(8,128)(2,1)}) fusion(bf16[8192,256]{0,1:T(8,128)(2,1)} %all-gather.3.cloned.1.call-done), kind=kLoop, calls=%fused_computation.68 | loop fusion | bytes 8388608 | tf_op jit(solution)/shard_map/split | solution.py:38
  195.0 4.1 %copy.51 = bf16[8192,128]{1,0:T(8,128)(2,1)} copy(bf16[8192,128]{0,1:T(8,128)(2,1)} %get-tuple-element.337) | data formatting | bytes 4194304
  199.1 4.1 %copy.54 = bf16[8192,128]{1,0:T(8,128)(2,1)} copy(bf16[8192,128]{0,1:T(8,128)(2,1)} %get-tuple-element.336) | data formatting | bytes 4194304
  203.2 86.8 %while.17 = (s32[]{:T(128)}, f32[1,2048]{1,0:T(1,128)S(1)}, f32[1,2048]{1,0:T(1,128)S(1)}, f32[1,2048,128]{2,1,0:T(8,128)S(1)}, s32[8,1024]{1,0:T(8,128)S(1)}, /...) while((s32[]{:T(128)}, f32[1,2048]{1,0:T(1,128)S(1)}, ...), condition=%wide.region_9.10_spmd.clone, body=%wide.region_3.9_spmd.clone.sunk | while | flops 1107825664 | bytes 28514564 | solution.py:181
  203.3 0.6 fusion.51
  205.1 9.0 %conditional.3 = ((f32[1,2048]{1,0:T(1,128)S(1)}, f32[1,2048]{1,0:T(1,128)S(1)}, f32[1,2048,128]{2,1,0:T(8,128)S(1)})) conditional(s32[]{:T(128)} %convert_element_type.119, (f32[1,2048]{1,0:T(1,128)S(1)}, f32[1,2048]{1,0:T(1,128)S(1)}, f32[1,2048,128]{2,1,0:T(8,128)S(1)}) %tuple.64, (s32[1,1024]{1,0:T(1,128)S(1)}, s32[256]{0:T(256)S(1)}, ...), branch_computations={%region_5.5_spmd, %region_6.8_spmd} | conditional | flops 1107824640 | bytes 28506144 | solution.py:141
  205.1 2.5 fusion.2
  207.6 2.7 fusion.4
  210.3 3.7 %fusion.10 = f32[1,2048,128]{2,1,0:T(8,128)S(1)} fusion(f32[1024,2048]{1,0:T(8,128)S(1)} %get-tuple-element.335, f32[2048]{0:T(1024)S(1)} %bitcast.88, s32[2048]{0:T(1024)S(1)} %bitcast.96, s32[1024]{0:T(1024)S(1)} %bitcast.101, f32[1,2048,128]{2,1,0:T(8,128)S(1)} %get-tuple-element.191, f32[2048]{0:T(1024)S(1)} %bitcast.104, ...), kind=kOutput, calls=%fused_computation.8 | convolution fusion | flops 549978112 | bytes 10777088 | tf_op jit(solution)/shard_map/while/body/eval_jaxpr/cond/branch_1_fun/hqk,khe->hqe/dot_general | solution.py:131
  214.1 0.6 fusion.51
  215.9 9.0 %conditional.3 = ((f32[1,2048]{1,0:T(1,128)S(1)}, f32[1,2048]{1,0:T(1,128)S(1)}, f32[1,2048,128]{2,1,0:T(8,128)S(1)})) conditional(s32[]{:T(128)} %convert_element_type.119, (f32[1,2048]{1,0:T(1,128)S(1)}, f32[1,2048]{1,0:T(1,128)S(1)}, f32[1,2048,128]{2,1,0:T(8,128)S(1)}) %tuple.64, (s32[1,1024]{1,0:T(1,128)S(1)}, s32[256]{0:T(256)S(1)}, ...), branch_computations={%region_5.5_spmd, %region_6.8_spmd} | conditional | flops 1107824640 | bytes 28506144 | solution.py:141
  215.9 2.5 fusion.2
  218.4 2.7 fusion.4
  221.1 3.7 %fusion.10 = f32[1,2048,128]{2,1,0:T(8,128)S(1)} fusion(f32[1024,2048]{1,0:T(8,128)S(1)} %get-tuple-element.335, f32[2048]{0:T(1024)S(1)} %bitcast.88, s32[2048]{0:T(1024)S(1)} %bitcast.96, s32[1024]{0:T(1024)S(1)} %bitcast.101, f32[1,2048,128]{2,1,0:T(8,128)S(1)} %get-tuple-element.191, f32[2048]{0:T(1024)S(1)} %bitcast.104, ...), kind=kOutput, calls=%fused_computation.8 | convolution fusion | flops 549978112 | bytes 10777088 | tf_op jit(solution)/shard_map/while/body/eval_jaxpr/cond/branch_1_fun/hqk,khe->hqe/dot_general | solution.py:131
  224.9 0.6 fusion.51
  226.7 9.0 %conditional.3 = ((f32[1,2048]{1,0:T(1,128)S(1)}, f32[1,2048]{1,0:T(1,128)S(1)}, f32[1,2048,128]{2,1,0:T(8,128)S(1)})) conditional(s32[]{:T(128)} %convert_element_type.119, (f32[1,2048]{1,0:T(1,128)S(1)}, f32[1,2048]{1,0:T(1,128)S(1)}, f32[1,2048,128]{2,1,0:T(8,128)S(1)}) %tuple.64, (s32[1,1024]{1,0:T(1,128)S(1)}, s32[256]{0:T(256)S(1)}, ...), branch_computations={%region_5.5_spmd, %region_6.8_spmd} | conditional | flops 1107824640 | bytes 28506144 | solution.py:141
  226.8 2.5 fusion.2
  229.2 2.7 fusion.4
  231.9 3.7 %fusion.10 = f32[1,2048,128]{2,1,0:T(8,128)S(1)} fusion(f32[1024,2048]{1,0:T(8,128)S(1)} %get-tuple-element.335, f32[2048]{0:T(1024)S(1)} %bitcast.88, s32[2048]{0:T(1024)S(1)} %bitcast.96, s32[1024]{0:T(1024)S(1)} %bitcast.101, f32[1,2048,128]{2,1,0:T(8,128)S(1)} %get-tuple-element.191, f32[2048]{0:T(1024)S(1)} %bitcast.104, ...), kind=kOutput, calls=%fused_computation.8 | convolution fusion | flops 549978112 | bytes 10777088 | tf_op jit(solution)/shard_map/while/body/eval_jaxpr/cond/branch_1_fun/hqk,khe->hqe/dot_general | solution.py:131
  235.7 0.6 fusion.51
  237.5 9.0 %conditional.3 = ((f32[1,2048]{1,0:T(1,128)S(1)}, f32[1,2048]{1,0:T(1,128)S(1)}, f32[1,2048,128]{2,1,0:T(8,128)S(1)})) conditional(s32[]{:T(128)} %convert_element_type.119, (f32[1,2048]{1,0:T(1,128)S(1)}, f32[1,2048]{1,0:T(1,128)S(1)}, f32[1,2048,128]{2,1,0:T(8,128)S(1)}) %tuple.64, (s32[1,1024]{1,0:T(1,128)S(1)}, s32[256]{0:T(256)S(1)}, ...), branch_computations={%region_5.5_spmd, %region_6.8_spmd} | conditional | flops 1107824640 | bytes 28506144 | solution.py:141
  237.6 2.5 fusion.2
  240.1 2.7 fusion.4
  242.8 3.7 %fusion.10 = f32[1,2048,128]{2,1,0:T(8,128)S(1)} fusion(f32[1024,2048]{1,0:T(8,128)S(1)} %get-tuple-element.335, f32[2048]{0:T(1024)S(1)} %bitcast.88, s32[2048]{0:T(1024)S(1)} %bitcast.96, s32[1024]{0:T(1024)S(1)} %bitcast.101, f32[1,2048,128]{2,1,0:T(8,128)S(1)} %get-tuple-element.191, f32[2048]{0:T(1024)S(1)} %bitcast.104, ...), kind=kOutput, calls=%fused_computation.8 | convolution fusion | flops 549978112 | bytes 10777088 | tf_op jit(solution)/shard_map/while/body/eval_jaxpr/cond/branch_1_fun/hqk,khe->hqe/dot_general | solution.py:131
  248.4 9.0 %conditional.3 = ((f32[1,2048]{1,0:T(1,128)S(1)}, f32[1,2048]{1,0:T(1,128)S(1)}, f32[1,2048,128]{2,1,0:T(8,128)S(1)})) conditional(s32[]{:T(128)} %convert_element_type.119, (f32[1,2048]{1,0:T(1,128)S(1)}, f32[1,2048]{1,0:T(1,128)S(1)}, f32[1,2048,128]{2,1,0:T(8,128)S(1)}) %tuple.64, (s32[1,1024]{1,0:T(1,128)S(1)}, s32[256]{0:T(256)S(1)}, ...), branch_computations={%region_5.5_spmd, %region_6.8_spmd} | conditional | flops 1107824640 | bytes 28506144 | solution.py:141
  248.4 2.5 fusion.2
  250.9 2.7 fusion.4
  253.6 3.7 %fusion.10 = f32[1,2048,128]{2,1,0:T(8,128)S(1)} fusion(f32[1024,2048]{1,0:T(8,128)S(1)} %get-tuple-element.335, f32[2048]{0:T(1024)S(1)} %bitcast.88, s32[2048]{0:T(1024)S(1)} %bitcast.96, s32[1024]{0:T(1024)S(1)} %bitcast.101, f32[1,2048,128]{2,1,0:T(8,128)S(1)} %get-tuple-element.191, f32[2048]{0:T(1024)S(1)} %bitcast.104, ...), kind=kOutput, calls=%fused_computation.8 | convolution fusion | flops 549978112 | bytes 10777088 | tf_op jit(solution)/shard_map/while/body/eval_jaxpr/cond/branch_1_fun/hqk,khe->hqe/dot_general | solution.py:131
  259.2 9.0 %conditional.3 = ((f32[1,2048]{1,0:T(1,128)S(1)}, f32[1,2048]{1,0:T(1,128)S(1)}, f32[1,2048,128]{2,1,0:T(8,128)S(1)})) conditional(s32[]{:T(128)} %convert_element_type.119, (f32[1,2048]{1,0:T(1,128)S(1)}, f32[1,2048]{1,0:T(1,128)S(1)}, f32[1,2048,128]{2,1,0:T(8,128)S(1)}) %tuple.64, (s32[1,1024]{1,0:T(1,128)S(1)}, s32[256]{0:T(256)S(1)}, ...), branch_computations={%region_5.5_spmd, %region_6.8_spmd} | conditional | flops 1107824640 | bytes 28506144 | solution.py:141
  259.2 2.5 fusion.2
  261.7 2.7 fusion.4
  264.4 3.7 %fusion.10 = f32[1,2048,128]{2,1,0:T(8,128)S(1)} fusion(f32[1024,2048]{1,0:T(8,128)S(1)} %get-tuple-element.335, f32[2048]{0:T(1024)S(1)} %bitcast.88, s32[2048]{0:T(1024)S(1)} %bitcast.96, s32[1024]{0:T(1024)S(1)} %bitcast.101, f32[1,2048,128]{2,1,0:T(8,128)S(1)} %get-tuple-element.191, f32[2048]{0:T(1024)S(1)} %bitcast.104, ...), kind=kOutput, calls=%fused_computation.8 | convolution fusion | flops 549978112 | bytes 10777088 | tf_op jit(solution)/shard_map/while/body/eval_jaxpr/cond/branch_1_fun/hqk,khe->hqe/dot_general | solution.py:131
  270.0 9.0 %conditional.3 = ((f32[1,2048]{1,0:T(1,128)S(1)}, f32[1,2048]{1,0:T(1,128)S(1)}, f32[1,2048,128]{2,1,0:T(8,128)S(1)})) conditional(s32[]{:T(128)} %convert_element_type.119, (f32[1,2048]{1,0:T(1,128)S(1)}, f32[1,2048]{1,0:T(1,128)S(1)}, f32[1,2048,128]{2,1,0:T(8,128)S(1)}) %tuple.64, (s32[1,1024]{1,0:T(1,128)S(1)}, s32[256]{0:T(256)S(1)}, ...), branch_computations={%region_5.5_spmd, %region_6.8_spmd} | conditional | flops 1107824640 | bytes 28506144 | solution.py:141
  270.0 2.5 fusion.2
  272.5 2.7 fusion.4
  275.2 3.7 %fusion.10 = f32[1,2048,128]{2,1,0:T(8,128)S(1)} fusion(f32[1024,2048]{1,0:T(8,128)S(1)} %get-tuple-element.335, f32[2048]{0:T(1024)S(1)} %bitcast.88, s32[2048]{0:T(1024)S(1)} %bitcast.96, s32[1024]{0:T(1024)S(1)} %bitcast.101, f32[1,2048,128]{2,1,0:T(8,128)S(1)} %get-tuple-element.191, f32[2048]{0:T(1024)S(1)} %bitcast.104, ...), kind=kOutput, calls=%fused_computation.8 | convolution fusion | flops 549978112 | bytes 10777088 | tf_op jit(solution)/shard_map/while/body/eval_jaxpr/cond/branch_1_fun/hqk,khe->hqe/dot_general | solution.py:131
  280.8 9.0 %conditional.3 = ((f32[1,2048]{1,0:T(1,128)S(1)}, f32[1,2048]{1,0:T(1,128)S(1)}, f32[1,2048,128]{2,1,0:T(8,128)S(1)})) conditional(s32[]{:T(128)} %convert_element_type.119, (f32[1,2048]{1,0:T(1,128)S(1)}, f32[1,2048]{1,0:T(1,128)S(1)}, f32[1,2048,128]{2,1,0:T(8,128)S(1)}) %tuple.64, (s32[1,1024]{1,0:T(1,128)S(1)}, s32[256]{0:T(256)S(1)}, ...), branch_computations={%region_5.5_spmd, %region_6.8_spmd} | conditional | flops 1107824640 | bytes 28506144 | solution.py:141
  280.9 2.5 fusion.2
  283.3 2.7 fusion.4
  286.0 3.7 %fusion.10 = f32[1,2048,128]{2,1,0:T(8,128)S(1)} fusion(f32[1024,2048]{1,0:T(8,128)S(1)} %get-tuple-element.335, f32[2048]{0:T(1024)S(1)} %bitcast.88, s32[2048]{0:T(1024)S(1)} %bitcast.96, s32[1024]{0:T(1024)S(1)} %bitcast.101, f32[1,2048,128]{2,1,0:T(8,128)S(1)} %get-tuple-element.191, f32[2048]{0:T(1024)S(1)} %bitcast.104, ...), kind=kOutput, calls=%fused_computation.8 | convolution fusion | flops 549978112 | bytes 10777088 | tf_op jit(solution)/shard_map/while/body/eval_jaxpr/cond/branch_1_fun/hqk,khe->hqe/dot_general | solution.py:131
  290.0 1.1 divide_convert_fusion
  291.2 1.2 copy.49
  292.4 7.1 %convolution_convert_fusion.1 = bf16[256,4096]{1,0:T(8,128)(2,1)} fusion(bf16[256,1024]{0,1:T(8,128)(2,1)S(1)} %bitcast.89, bf16[1024,4096]{1,0:T(8,128)(2,1)} %param.19), kind=kOutput, calls=%fused_computation.25 | convolution fusion | flops 2148532224 | bytes 11010048 | tf_op jit(solution)/shard_map/dot_general | solution.py:188
  299.5 4.4 %all-to-all-start.1 = ((bf16[4,64,4096]{2,1,0:T(8,128)(2,1)}), bf16[4,64,4096]{2,1,0:T(8,128)(2,1)}, u32[]{:S(2)}, u32[]{:S(2)}) async-start(bf16[4,64,4096]{2,1,0:T(8,128)(2,1)} %bitcast.84), calls=%async_computation.1 | async-start | bytes 4194304 | tf_op jit(solution)/shard_map/all_to_all | solution.py:49
  305.0 1.6 copy.55
  306.6 24.6 %all-to-all-done.1 = bf16[4,64,4096]{2,1,0:T(8,128)(2,1)} async-done(((bf16[4,64,4096]{2,1,0:T(8,128)(2,1)}), bf16[4,64,4096]{2,1,0:T(8,128)(2,1)}, u32[]{:S(2)}, u32[]{:S(2)}) %all-to-all-start.1) | async-done | bytes 2097184 | tf_op jit(solution)/shard_map/all_to_all | solution.py:49
  331.2 2.0 convert_reduce_fusion
  333.2 2.2 add_convert_fusion
  (81 shorter events, 6.9 us)
Async XLA Ops:
  6.5 46.1 %copy-start = (bf16[4096,128]{1,0:T(8,128)(2,1)S(1)}, bf16[4096,128]{1,0:T(8,128)(2,1)}, u32[]{:S(2)}) copy-start(bf16[4096,128]{1,0:T(8,128)(2,1)} %param.17) | copy-start | bytes 3145732
  6.5 4.9 %copy-start.4 = (s32[2]{0:T(128)S(1)}, s32[2]{0:T(128)}, u32[]{:S(2)}) copy-start(s32[2]{0:T(128)} %param.13) | copy-start | bytes 28
  14.5 6.6 %copy-start.3 = (f32[4096]{0:T(1024)S(1)}, f32[4096]{0:T(1024)}, u32[]{:S(2)}) copy-start(f32[4096]{0:T(1024)} %param.15) | copy-start | bytes 49156
  16.5 31.7 %all-to-all-start = ((bf16[4,256,1024]{2,1,0:T(8,128)(2,1)}), bf16[4,256,1024]{2,1,0:T(8,128)(2,1)}, u32[]{:S(2)}, u32[]{:S(2)}) async-start(bf16[4,256,1024]{2,1,0:T(8,128)(2,1)} %broadcast_in_dim.17), calls=%async_computation | async-start | bytes 4194304 | tf_op jit(solution)/shard_map/all_to_all | solution.py:25
  21.0 30.9 %copy-start.2 = (f32[4096]{0:T(1024)S(1)}, f32[4096]{0:T(1024)}, u32[]{:S(2)}) copy-start(f32[4096]{0:T(1024)} %param.14) | copy-start | bytes 49156
  21.0 169.4 %all-gather.3.cloned.1.call-start = ((), (), s32[]{:S(2)}) async-start(), calls=%async_computation.2 | async-start | bytes 4325376 | tf_op jit(solution)/shard_map/all_gather | solution.py:37
  51.8 1.4 copy-start.5
  299.5 31.7 %all-to-all-start.1 = ((bf16[4,64,4096]{2,1,0:T(8,128)(2,1)}), bf16[4,64,4096]{2,1,0:T(8,128)(2,1)}, u32[]{:S(2)}, u32[]{:S(2)}) async-start(bf16[4,64,4096]{2,1,0:T(8,128)(2,1)} %bitcast.84), calls=%async_computation.1 | async-start | bytes 4194304 | tf_op jit(solution)/shard_map/all_to_all | solution.py:49
  304.4 31.0 %copy-start.1 = (bf16[4096,128]{1,0:T(8,128)(2,1)S(1)}, bf16[4096,128]{1,0:T(8,128)(2,1)}, u32[]{:S(2)}) copy-start(bf16[4096,128]{1,0:T(8,128)(2,1)} %param.17) | copy-start | bytes 3145732
Sparse Core Ops, SparseCore 0:
  54.9 135.4 all-gather.2
where the time goes:
time: 344 us; the launch traced here: 342 us
  waiting for transfers between devices  95.4 us (28%)
  blocking collectives  71.9 us (21%)
  matrix products  66.4 us (19%)
  local copies, waits for them, and re-layouts  38.5 us (11%)
  other arithmetic  37 us (11%)
  between operations  13.7 us (4%)
  loops' own time  10.4 us (3%)
  starting transfers between devices  8.92 us (3%)
    all_gather x1, blocking collectives, on_device(): lax.all_gather(positions, 'ctx', axis=0, tiled=True)  71.9 us
    all_gather x1, waiting for transfers between devices, sent_together(): result = lax.all_gather(both, axis, axis=dim, tiled=True)  43.7 us
    dot_general x8, matrix products, fold_block(): jnp.einsum('hqk,khe->hqe', expd.astype(jnp.bfloat16), per_head_values, pr...  29.9 us
    all_to_all x1, waiting for transfers between devices, sent_to_all(): lax.all_to_all(jnp.broadcast_to(value[None], (devices, *value.shape)), ax...  27.1 us
    all_to_all x1, waiting for transfers between devices, sent_and_summed(): lax.all_to_all(parts, axis, split_axis=0, concat_axis=0, tiled=True)  24.6 us
    reduce_sum x8, other arithmetic, fold_block(): total = total * shrink + jnp.sum(expd, axis=2)  21.3 us
    dot_general x8, matrix products, fold_block(): jnp.einsum('hqe,khe->hqk', query_group, per_head_keys, preferred_element_...  19.6 us
    dot_general x1, local copies, waits for them, and re-layouts, on_device(): jnp.dot(normed, w_query, preferred_element_type=jnp.float32)  11.2 us
  transfers between devices with their start and end apart: 3, of which 3 were waited for; matrix products, arithmetic and copies ran while one was open for 7% of the time, Pallas kernels for 0%

commit v1 on v0

v1 whole, which is shorter than its diff:
```python
import math

import jax
import jax.numpy as jnp
from jax import lax
from jax.experimental import pallas as pl
from jax.experimental.pallas import tpu as pltpu
from jax.sharding import PartitionSpec as P

HEAD = 128
BLK = 128
MESH = pl.DeviceIdType.MESH
BF = jnp.bfloat16
F32 = jnp.float32

rope_base = 500000.0
norm_eps = 1e-05
LOW = -1e30


def dot(a, b):
    return jnp.dot(a, b, preferred_element_type=F32)


def layer_kernel(
    own, cosf, sinf, gain, router, wq_hbm, wk_hbm, wv_hbm, wo_hbm,
    out,
    wq, wkv, wo, part, zsame, zother, rel_p, rel_m,
    qacc, kvacc, ssq, gsum, q, buf_a, buf_b, m_ref, acc, att,
    prem, ploc, d_out, d_in, dl_out, dl_in, zs_out, zr_rel, zr_in,
    ssem, rsem, wsem,
):
    c = lax.axis_index("ctx")
    t = lax.axis_index("tp")
    x, zlo, y = c // 8, (c // 4) % 2, c % 4
    zhi, core = t // 2, t % 2
    z = zhi * 2 + zlo
    d = own.shape[2]
    half = d // 2
    heads = q.shape[0] // 256
    width = wo.shape[1]
    nchunk = width // d

    def dev(dx=0, dy=0, dz=0, dc=0):
        nx, ny, nz = (x + dx + 4) % 4, (y + dy + 4) % 4, (z + dz + 4) % 4
        return (nx * 8 + (nz % 2) * 4 + ny, (nz // 2) * 2 + (core + dc) % 2)

    right_x, left_x = dev(dx=1), dev(dx=-1)
    right_y, left_y = dev(dy=1), dev(dy=-1)
    up, down = dev(dz=1), dev(dz=-1)
    mate = dev(dc=1)
    zpair = (x * 8 + (1 - zlo) * 4 + y, t)

    wcopies = [
        pltpu.make_async_copy(wq_hbm, wq, wsem.at[0]),
        pltpu.make_async_copy(wk_hbm, wkv.at[:, 0:HEAD], wsem.at[1]),
        pltpu.make_async_copy(wv_hbm, wkv.at[:, HEAD : 2 * HEAD], wsem.at[2]),
        pltpu.make_async_copy(wo_hbm, wo, wsem.at[3]),
    ]
    for copy in wcopies:
        copy.start()

    barrier = pltpu.get_barrier_semaphore()
    for peer in (mate, up, down, right_x, left_x, right_y, left_y):
        pl.semaphore_signal(barrier, inc=1, device_id=peer, device_id_type=MESH)
    pl.semaphore_wait(barrier, 7)

    made = []

    def copy_to(src, dst, peer):
        k = len(made)
        copy = pltpu.make_async_remote_copy(
            src_ref=src, dst_ref=dst, send_sem=ssem.at[k], recv_sem=rsem.at[k],
            device_id=peer, device_id_type=MESH,
        )
        made.append(copy)
        return copy

    to_mate = [copy_to(own.at[b], part.at[b], mate) for b in range(2)]
    to_up = [copy_to(own.at[b, :, 0:half], rel_p.at[b], up) for b in range(2)]
    to_down = [copy_to(own.at[b, :, half:d], rel_m.at[b], down) for b in range(2)]
    fwd_up = [copy_to(rel_p.at[b], zsame.at[b, :, 0:half], up) for b in range(2)]
    fwd_down = [copy_to(rel_m.at[b], zsame.at[b, :, half:d], down) for b in range(2)]
    fwd_mate = [copy_to(zsame.at[b], zother.at[b], mate) for b in range(2)]
    for b in range(2):
        to_up[b].start()
        to_down[b].start()
        to_mate[b].start()

    ssq[...] = jnp.zeros_like(ssq)
    gsum[...] = jnp.zeros_like(gsum)
    src_own, src_mate = t, t + 1 - 2 * core
    src_same = (t + 2) % 4
    src_other = (src_mate + 2) % 4

    def project(ref, b, s, first):
        at = pl.multiple_of(s * d, d)
        rows = pl.ds(at, d)
        ch = ref[b].astype(F32)
        ssq[b] += jnp.broadcast_to(jnp.sum(ch * ch, axis=1, keepdims=True), (BLK, HEAD))
        gsum[b] += jnp.broadcast_to(
            jnp.sum(ch * router[:, rows], axis=1, keepdims=True), (BLK, HEAD)
        )
        cg = (ch * gain[:, rows]).astype(BF)
        pq = dot(cg, wq[rows, :])
        pkv = dot(cg, wkv[rows, :])
        if first:
            qacc[b] = pq
            kvacc[b] = pkv
        else:
            qacc[b] += pq
            kvacc[b] += pkv

    for copy in wcopies[:3]:
        copy.wait()
    for b in range(2):
        project(own, b, src_own, True)
    for b in range(2):
        to_up[b].wait_recv()
        fwd_up[b].start()
        to_down[b].wait_recv()
        fwd_down[b].start()
        if b == 0:
            for bb in range(2):
                to_mate[bb].wait_recv()
                project(part, bb, src_mate, False)
    for b in range(2):
        fwd_up[b].wait_recv()
        fwd_down[b].wait_recv()
        fwd_mate[b].start()
        project(zsame, b, src_same, False)
    for b in range(2):
        fwd_mate[b].wait_recv()
        project(zother, b, src_other, False)

    def rotated(v, b):
        return v * cosf[b] + pltpu.roll(v, HEAD // 2, 1) * sinf[b]

    def unit_at(buf, i, j, k):
        return buf.at[i, pl.ds(pl.multiple_of((j * 2 + k) * BLK, BLK), BLK)]

    def pair_at(buf, i, j):
        return buf.at[i, pl.ds(pl.multiple_of(j * 2 * BLK, 2 * BLK), 2 * BLK)]

    own_a = unit_at(buf_a, y, x, zlo)
    own_b = unit_at(buf_b, x, y, zlo)
    scale = math.log2(math.e) / math.sqrt(HEAD)
    for b, unit in ((0, own_a), (1, own_b)):
        inv = lax.rsqrt(ssq[b][:, 0:1] * (1.0 / width) + norm_eps)
        kv = kvacc[b] * inv
        unit[:, 0:HEAD] = rotated(kv[:, 0:HEAD], b).astype(BF)
        unit[:, HEAD : 2 * HEAD] = kv[:, HEAD:].astype(BF)

    class Side:
        pass

    def side(buf, i, j, plus1, minus1, plus2, minus2):
        s = Side()
        s.buf, s.i, s.j = buf, i, j
        own_unit = unit_at(buf, i, j, zlo)
        s.to_z = copy_to(own_unit, own_unit, zpair)
        z_unit = unit_at(buf, i, j, 1 - zlo)
        s.own_p = copy_to(own_unit, own_unit, plus1)
        s.own_m = copy_to(own_unit, own_unit, minus1)
        s.z_p = copy_to(z_unit, z_unit, plus1)
        s.z_m = copy_to(z_unit, z_unit, minus1)
        jm, jp = (j + 3) % 4, (j + 1) % 4
        s.rel_p = copy_to(unit_at(buf, i, jm, 0), unit_at(buf, i, jm, 0), plus1)
        s.rel_m = copy_to(unit_at(buf, i, jp, 1), unit_at(buf, i, jp, 1), minus1)
        s.order = (j, jm, jp, (j + 2) % 4)
        s.pair_p = [copy_to(pair_at(buf, i, k), pair_at(buf, i, k), plus2) for k in s.order]
        s.pair_m = [copy_to(pair_at(buf, i, k), pair_at(buf, i, k), minus2) for k in s.order]
        im, ip = (i + 3) % 4, (i + 1) % 4
        s.im, s.ip, s.io = im, ip, (i + 2) % 4
        s.opp_p = [copy_to(unit_at(buf, im, k, 0), unit_at(buf, im, k, 0), plus2) for k in s.order]
        s.opp_m = [copy_to(unit_at(buf, ip, k, 1), unit_at(buf, ip, k, 1), minus2) for k in s.order]
        return s

    side_a = side(buf_a, y, x, right_x, left_x, right_y, left_y)
    side_b = side(buf_b, x, y, right_y, left_y, right_x, left_x)
    sides = (side_a, side_b)

    for s in sides:
        s.to_z.start()
        s.own_p.start()
        s.own_m.start()

    for b in range(2):
        inv = lax.rsqrt(ssq[b][:, 0:1] * (1.0 / width) + norm_eps)
        for h in range(heads):
            qh = qacc[b][:, h * HEAD : (h + 1) * HEAD] * inv
            q[h * 256 + b * BLK : h * 256 + (b + 1) * BLK, :] = (
                rotated(qh, b) * scale
            ).astype(BF)

    for s in sides:
        s.to_z.wait_recv()
        s.z_p.start()
        s.z_m.start()
        s.pair_p[0].start()
        s.pair_m[0].start()

    ones_own = jnp.ones((2 * BLK, HEAD), BF)
    keys_own = jnp.concatenate([own_a[...], own_b[...]], axis=0)
    k_own = keys_own[:, 0:HEAD]
    v_own = jnp.concatenate([keys_own[:, HEAD:], ones_own], axis=1)
    row_at = lax.broadcasted_iota(jnp.int32, (256, 256), 0)
    col_at = lax.broadcasted_iota(jnp.int32, (256, 256), 1)
    lower = col_at <= row_at

    def scores_of(qs, ks):
        return lax.dot_general(qs, ks, (((1,), (1,)), ((), ())), preferred_element_type=F32)

    def own_head(h, carry):
        rows = pl.ds(pl.multiple_of(h * 256, 256), 256)
        sc = jnp.where(lower, scores_of(q[rows, :], k_own), LOW)
        high = jnp.max(sc, axis=1, keepdims=True)
        pr = jnp.where(lower, jnp.exp2(sc - high), 0.0).astype(BF)
        m_ref[rows, :] = jnp.broadcast_to(high, (256, HEAD))
        acc[rows, :] = dot(pr, v_own)
        return carry

    lax.fori_loop(0, heads, own_head, 0)

    keys = 8 * BLK
    step_rows = 256

    def attend(buf, g, n, rank_of):
        @pl.when(n > 0)
        def _():
            def rows_step(r, carry):
                rows = pl.ds(pl.multiple_of(r * step_rows, step_rows), step_rows)
                unit_of = lax.broadcasted_iota(jnp.int32, (1, keys), 1) >> 7
                bias = jnp.where(rank_of(unit_of) < n, 0.0, LOW)
                kk = buf[g, :, 0:HEAD]
                vv = jnp.concatenate([buf[g, :, HEAD:], jnp.ones((keys, HEAD), BF)], axis=1)
                sc = scores_of(q[rows, :], kk) + bias
                old = m_ref[rows, :]
                high = jnp.maximum(old, jnp.max(sc, axis=1, keepdims=True))
                pr = jnp.exp2(sc - jnp.concatenate([high] * 8, axis=1)).astype(BF)
                shrink = jnp.exp2(old - high)
                m_ref[rows, :] = high
                acc[rows, :] = acc[rows, :] * jnp.concatenate([shrink] * 2, axis=1) + dot(pr, vv)
                return carry

            lax.fori_loop(0, q.shape[0] // step_rows, rows_step, 0)

    def attend_a(g):
        attend(buf_a, g, x * 2 + zlo + jnp.where(g < y, 1, 0), lambda u: u)

    def attend_b(g):
        count = jnp.where(g < x, 8, jnp.where(g == x, zlo * 4 + y, 0))
        attend(buf_b, g, count, lambda u: (u & 1) * 4 + (u >> 1))

    for s in sides:
        s.own_p.wait_recv()
        s.z_p.wait_recv()
        s.rel_p.start()
        s.own_m.wait_recv()
        s.z_m.wait_recv()
        s.rel_m.start()
        for k in (1, 2):
            s.pair_p[k].start()
            s.pair_m[k].start()
    for s in sides:
        s.rel_p.wait_recv()
        s.rel_m.wait_recv()
        s.pair_p[3].start()
        s.pair_m[3].start()

    def relay(k):
        for s in sides:
            s.pair_p[k].wait_recv()
            s.opp_p[k].start()
            s.pair_m[k].wait_recv()
            s.opp_m[k].start()

    relay(0)
    attend_a(side_a.i)
    relay(1)
    attend_b(side_b.i)
    relay(2)
    relay(3)
    attend_a(side_a.im)
    attend_a(side_a.ip)
    attend_b(side_b.im)
    attend_b(side_b.ip)
    for k in range(4):
        side_a.opp_p[k].wait_recv()
        side_a.opp_m[k].wait_recv()
    attend_a(side_a.io)
    for k in range(4):
        side_b.opp_p[k].wait_recv()
        side_b.opp_m[k].wait_recv()
    attend_b(side_b.io)

    for h in range(heads):
        rows = slice(h * 256, (h + 1) * 256)
        att[:, h * HEAD : (h + 1) * HEAD] = (
            acc[rows, 0:HEAD] / acc[rows, HEAD : 2 * HEAD]
        ).astype(BF)

    wcopies[3].wait()
    piece = BLK // 2
    mine = pl.ds(pl.multiple_of(core * piece, piece), piece)
    other = pl.ds(pl.multiple_of((1 - core) * piece, piece), piece)
    far_rows = pl.ds(pl.multiple_of((1 - zhi) * BLK, BLK), BLK)
    near_rows = pl.ds(pl.multiple_of(zhi * BLK, BLK), BLK)
    order = (0, 2, 1, 3)
    far_mate = [copy_to(d_out.at[j], d_in.at[j], mate) for j in range(4)]
    near_mate = [copy_to(dl_out.at[j], dl_in.at[j], mate) for j in range(4)]
    first_hop = [
        copy_to(zs_out.at[j], zr_rel.at[j], up if j < 2 else down) for j in range(4)
    ]
    second_hop = [
        copy_to(zr_rel.at[j], zr_in.at[j], up if j < 2 else down) for j in range(4)
    ]

    def pass_on(j):
        far_mate[j].wait_recv()
        zs_out[j] = (prem[j, mine, :] + d_in[j].astype(F32)).astype(BF)
        first_hop[j].start()

    last = None
    for j in order:
        prem[j] = dot(att[far_rows, :], wo[:, j * d : (j + 1) * d])
        d_out[j] = prem[j, other, :].astype(BF)
        far_mate[j].start()
        if last is not None:
            pass_on(last)
        last = j
    pass_on(last)
    for k, j in enumerate(order):
        ploc[j] = dot(att[near_rows, :], wo[:, j * d : (j + 1) * d])
        dl_out[j] = ploc[j, other, :].astype(BF)
        near_mate[j].start()
    for j in order:
        first_hop[j].wait_recv()
        second_hop[j].start()
    for j in order:
        near_mate[j].wait_recv()
        ploc[j, mine, :] += dl_in[j].astype(F32)

    gate = 1.0 / (1.0 + jnp.exp(-gsum[zhi, mine, 0:1]))
    for j in order:
        second_hop[j].wait_recv()
    for ref, s in ((own, src_own), (part, src_mate), (zsame, src_same), (zother, src_other)):
        total = ploc[s, mine, :] + zr_in[s].astype(F32)
        out[s] = (ref[zhi, mine, :].astype(F32) + gate * total).astype(BF)

    for copy in made:
        copy.wait_send()


def on_device(resid, sel_blocks, norm_gain, router_weight, w_query, w_key, value_projection, w_out):
    local_rows, d = resid.shape
    width = w_out.shape[1]
    count = local_rows // BLK
    local_ids = sel_blocks - lax.axis_index("ctx") * count
    blocks = resid.reshape(count, BLK, d)
    own = jnp.concatenate(
        [lax.dynamic_slice_in_dim(blocks, local_ids[b], 1, 0) for b in range(2)], axis=0
    )
    positions = sel_blocks[:, None] * BLK + jnp.arange(BLK, dtype=jnp.int32)[None, :]
    freqs = jnp.exp(
        jnp.arange(HEAD // 2, dtype=F32) * (-2.0 * math.log(rope_base) / HEAD)
    )
    angles = positions.astype(F32)[:, :, None] * freqs[None, None, :]
    cosine, sine = jnp.cos(angles), jnp.sin(angles)
    cosf = jnp.concatenate([cosine, cosine], axis=2)
    sinf = jnp.concatenate([-sine, sine], axis=2)
    qcols = w_query.shape[1]
    heads = qcols // HEAD
    vmem = pl.BlockSpec(memory_space=pltpu.VMEM)
    anyspace = pl.BlockSpec(memory_space=pl.ANY)
    piece = BLK // 2
    nsem = 74
    result = pl.pallas_call(
        layer_kernel,
        name="layer",
        out_shape=jax.ShapeDtypeStruct((4, piece, d), BF),
        in_specs=[vmem] * 5 + [anyspace] * 4,
        out_specs=vmem,
        scratch_shapes=[
            pltpu.VMEM((width, qcols), BF),
            pltpu.VMEM((width, 2 * HEAD), BF),
            pltpu.VMEM((qcols, width), BF),
            pltpu.VMEM((2, BLK, d), BF),
            pltpu.VMEM((2, BLK, d), BF),
            pltpu.VMEM((2, BLK, d), BF),
            pltpu.VMEM((2, BLK, d // 2), BF),
            pltpu.VMEM((2, BLK, d // 2), BF),
            pltpu.VMEM((2, BLK, qcols), F32),
            pltpu.VMEM((2, BLK, 2 * HEAD), F32),
            pltpu.VMEM((2, BLK, HEAD), F32),
            pltpu.VMEM((2, BLK, HEAD), F32),
            pltpu.VMEM((heads * 256, HEAD), BF),
            pltpu.VMEM((4, 8 * BLK, 2 * HEAD), BF),
            pltpu.VMEM((4, 8 * BLK, 2 * HEAD), BF),
            pltpu.VMEM((heads * 256, HEAD), F32),
            pltpu.VMEM((heads * 256, 2 * HEAD), F32),
            pltpu.VMEM((256, qcols), BF),
            pltpu.VMEM((4, BLK, d), F32),
            pltpu.VMEM((4, BLK, d), F32),
            pltpu.VMEM((4, piece, d), BF),
            pltpu.VMEM((4, piece, d), BF),
            pltpu.VMEM((4, piece, d), BF),
            pltpu.VMEM((4, piece, d), BF),
            pltpu.VMEM((4, piece, d), BF),
            pltpu.VMEM((4, piece, d), BF),
            pltpu.VMEM((4, piece, d), BF),
            pltpu.SemaphoreType.DMA((nsem,)),
            pltpu.SemaphoreType.DMA((nsem,)),
            pltpu.SemaphoreType.DMA((4,)),
        ],
        compiler_params=pltpu.CompilerParams(
            collective_id=0, has_side_effects=True, vmem_limit_bytes=60 * 1024 * 1024
        ),
    )(
        own, cosf, sinf, norm_gain.reshape(1, width), router_weight.reshape(1, width),
        w_query, w_key, value_projection, w_out,
    )
    return result.transpose(1, 0, 2).reshape(piece, width)


def solution(mesh):
    return jax.shard_map(
        on_device,
        mesh=mesh,
        in_specs=(
            P("ctx", "tp"),
            P("ctx"),
            P(),
            P(),
            P(None, "tp"),
            P(None, "tp"),
            P(None, "tp"),
            P("tp", None),
        ),
        out_specs=P(("ctx", "tp"), None),
        check_vma=False,
    )
```

time: 344 us -> 123 us (0.36)
  the two profiles are of different devices: /device:TPU:46 before, /device:TPU:7 now
where the time goes in v1:
time: 123 us; the launch traced here: 122 us
  Pallas kernels  112 us (91%)
  between operations  3.82 us (3%)
  local copies, waits for them, and re-layouts  3.53 us (3%)
  other arithmetic  2.96 us (2%)
    pallas_call x1, Pallas kernels, on_device(): pl.pallas_call(layer_kernel, name='layer', out_shape=jax.ShapeDtypeStruct...  112 us

profile of v1, /device:TPU:7, one launch (start us, length us, event | category | flops | bytes accessed | tf_op | source)
XLA Modules:
  0.0 122.3 jit_solution(17771117775090479350)
XLA Ops:
  0.0 0.7 broadcast_multiply_fusion
  0.7 0.1 add_convert_fusion
  0.7 0.6 fusion.1
  5.1 0.5 fusion
  5.7 0.8 pad_maximum_fusion.1
  6.5 1.1 constant_dynamic-slice_fusion.1
  7.6 0.8 pad_maximum_fusion.own
  8.4 112.0 %layer.1 = bf16[4,64,1024]{2,1,0:T(8,128)(2,1)} custom-call(bf16[2,128,1024]{2,1,0:T(8,128)(2,1)} %pad_maximum_fusion.own, f32[2,128,128]{2,1,0:T(8,128)} %get-tuple-element.14.cosf, f32[2,128,128]{2,1,0:T(8,128)} %get-tuple-element.15.sinf, f32[1,4096]{1,0:T(1,128)} %bitcast.10, f32[1,4096]{1,0:T(1,128)} %bitcast.11, bf16[4096,1024]{1,0:T(8,128)(2,1)} %wq_hbm.1, ...), custom_call_target="tpu_custom_call" | custom-call | tf_op jit(solution)/shard_map/layer/pallas_call | solution.py:378
  120.5 1.9 %copy.10 = bf16[4,8,8,1024]{3,2,0,1:T(8,128)(2,1)} copy(bf16[4,8,8,1024]{3,2,1,0:T(8,128)(2,1)} %bitcast.8) | data formatting | bytes 1048576 | tf_op jit(solution)/shard_map/reshape | solution.py:423
  (1 shorter events, 0.0 us)

commit v2 on v1

--- a/solution.py
+++ b/solution.py
@@ -26,7 +26,7 @@
     own, cosf, sinf, gain, router, wq_hbm, wk_hbm, wv_hbm, wo_hbm,
     out,
     wq, wkv, wo, part, zsame, zother, rel_p, rel_m,
-    qacc, kvacc, ssq, gsum, q, buf_a, buf_b, m_ref, acc, att,
+    qacc, kvacc, ssq, gsum, q, buf, m_ref, acc, s_ref, p_ref, x_ref, att,
     prem, ploc, d_out, d_in, dl_out, dl_in, zs_out, zr_rel, zr_in,
     ssem, rsem, wsem,
 ):
@@ -136,48 +136,47 @@
     def rotated(v, b):
         return v * cosf[b] + pltpu.roll(v, HEAD // 2, 1) * sinf[b]
 
-    def unit_at(buf, i, j, k):
-        return buf.at[i, pl.ds(pl.multiple_of((j * 2 + k) * BLK, BLK), BLK)]
-
-    def pair_at(buf, i, j):
-        return buf.at[i, pl.ds(pl.multiple_of(j * 2 * BLK, 2 * BLK), 2 * BLK)]
-
-    own_a = unit_at(buf_a, y, x, zlo)
-    own_b = unit_at(buf_b, x, y, zlo)
+    def unit_at(base, i, j, k):
+        return buf.at[base + i, pl.ds(pl.multiple_of((j * 2 + k) * BLK, BLK), BLK)]
+
+    def pair_at(base, i, j):
+        return buf.at[base + i, pl.ds(pl.multiple_of(j * 2 * BLK, 2 * BLK), 2 * BLK)]
+
+    own_a = unit_at(0, y, x, zlo)
+    own_b = unit_at(4, x, y, zlo)
     scale = math.log2(math.e) / math.sqrt(HEAD)
     for b, unit in ((0, own_a), (1, own_b)):
         inv = lax.rsqrt(ssq[b][:, 0:1] * (1.0 / width) + norm_eps)
         kv = kvacc[b] * inv
         unit[:, 0:HEAD] = rotated(kv[:, 0:HEAD], b).astype(BF)
-        unit[:, HEAD : 2 * HEAD] = kv[:, HEAD:].astype(BF)
+        unit[:, HEAD : 2 * HEAD] = kv[:, HEAD:].T.astype(BF)
 
     class Side:
         pass
 
-    def side(buf, i, j, plus1, minus1, plus2, minus2):
+    def side(base, i, j, plus1, minus1, plus2, minus2):
         s = Side()
-        s.buf, s.i, s.j = buf, i, j
-        own_unit = unit_at(buf, i, j, zlo)
+        own_unit = unit_at(base, i, j, zlo)
         s.to_z = copy_to(own_unit, own_unit, zpair)
-        z_unit = unit_at(buf, i, j, 1 - zlo)
+        z_unit = unit_at(base, i, j, 1 - zlo)
         s.own_p = copy_to(own_unit, own_unit, plus1)
         s.own_m = copy_to(own_unit, own_unit, minus1)
         s.z_p = copy_to(z_unit, z_unit, plus1)
         s.z_m = copy_to(z_unit, z_unit, minus1)
         jm, jp = (j + 3) % 4, (j + 1) % 4
-        s.rel_p = copy_to(unit_at(buf, i, jm, 0), unit_at(buf, i, jm, 0), plus1)
-        s.rel_m = copy_to(unit_at(buf, i, jp, 1), unit_at(buf, i, jp, 1), minus1)
+        s.rel_p = copy_to(unit_at(base, i, jm, 0), unit_at(base, i, jm, 0), plus1)
+        s.rel_m = copy_to(unit_at(base, i, jp, 1), unit_at(base, i, jp, 1), minus1)
         s.order = (j, jm, jp, (j + 2) % 4)
-        s.pair_p = [copy_to(pair_at(buf, i, k), pair_at(buf, i, k), plus2) for k in s.order]
-        s.pair_m = [copy_to(pair_at(buf, i, k), pair_at(buf, i, k), minus2) for k in s.order]
+        s.pair_p = [copy_to(pair_at(base, i, k), pair_at(base, i, k), plus2) for k in s.order]
+        s.pair_m = [copy_to(pair_at(base, i, k), pair_at(base, i, k), minus2) for k in s.order]
         im, ip = (i + 3) % 4, (i + 1) % 4
-        s.im, s.ip, s.io = im, ip, (i + 2) % 4
-        s.opp_p = [copy_to(unit_at(buf, im, k, 0), unit_at(buf, im, k, 0), plus2) for k in s.order]
-        s.opp_m = [copy_to(unit_at(buf, ip, k, 1), unit_at(buf, ip, k, 1), minus2) for k in s.order]
+        s.i, s.im, s.ip, s.io = i, im, ip, (i + 2) % 4
+        s.opp_p = [copy_to(unit_at(base, im, k, 0), unit_at(base, im, k, 0), plus2) for k in s.order]
+        s.opp_m = [copy_to(unit_at(base, ip, k, 1), unit_at(base, ip, k, 1), minus2) for k in s.order]
         return s
 
-    side_a = side(buf_a, y, x, right_x, left_x, right_y, left_y)
-    side_b = side(buf_b, x, y, right_y, left_y, right_x, left_x)
+    side_a = side(0, y, x, right_x, left_x, right_y, left_y)
+    side_b = side(4, x, y, right_y, left_y, right_x, left_x)
     sides = (side_a, side_b)
 
     for s in sides:
@@ -200,57 +199,74 @@
         s.pair_p[0].start()
         s.pair_m[0].start()
 
-    ones_own = jnp.ones((2 * BLK, HEAD), BF)
-    keys_own = jnp.concatenate([own_a[...], own_b[...]], axis=0)
-    k_own = keys_own[:, 0:HEAD]
-    v_own = jnp.concatenate([keys_own[:, HEAD:], ones_own], axis=1)
-    row_at = lax.broadcasted_iota(jnp.int32, (256, 256), 0)
-    col_at = lax.broadcasted_iota(jnp.int32, (256, 256), 1)
-    lower = col_at <= row_at
-
-    def scores_of(qs, ks):
-        return lax.dot_general(qs, ks, (((1,), (1,)), ((), ())), preferred_element_type=F32)
-
-    def own_head(h, carry):
-        rows = pl.ds(pl.multiple_of(h * 256, 256), 256)
-        sc = jnp.where(lower, scores_of(q[rows, :], k_own), LOW)
-        high = jnp.max(sc, axis=1, keepdims=True)
-        pr = jnp.where(lower, jnp.exp2(sc - high), 0.0).astype(BF)
-        m_ref[rows, :] = jnp.broadcast_to(high, (256, HEAD))
-        acc[rows, :] = dot(pr, v_own)
-        return carry
-
-    lax.fori_loop(0, heads, own_head, 0)
-
-    keys = 8 * BLK
-    step_rows = 256
-
-    def attend(buf, g, n, rank_of):
+    cols = 512
+    tiles = heads * 256 // cols
+    ones_rows = jnp.ones((16, 8 * BLK), BF)
+
+    def scores_of(ks, r):
+        return lax.dot_general(
+            ks, q[r * cols : (r + 1) * cols, :], (((1,), (1,)), ((), ())),
+            preferred_element_type=F32,
+        )
+
+    keys_own = jnp.concatenate([own_a[:, 0:HEAD], own_b[:, 0:HEAD]], axis=0)
+    v_own = jnp.concatenate([own_a[:, HEAD:], own_b[:, HEAD:]], axis=1)
+    v_own = jnp.concatenate([v_own, ones_rows[:, 0 : 2 * BLK]], axis=0)
+    key_at = lax.broadcasted_iota(jnp.int32, (256, cols), 0)
+    query_at = lax.broadcasted_iota(jnp.int32, (256, cols), 1) & 255
+    upper = key_at <= query_at
+    for r in range(tiles):
+        at = slice(r * cols, (r + 1) * cols)
+        sc = jnp.where(upper, scores_of(keys_own, r), LOW)
+        high = jnp.max(sc, axis=0, keepdims=True)
+        pr = jnp.where(upper, jnp.exp2(sc - high), 0.0).astype(BF)
+        m_ref[:, at] = jnp.broadcast_to(high, (8, cols))
+        acc[:, at] = dot(v_own, pr)
+
+    def attend(g, n, rank):
         @pl.when(n > 0)
         def _():
-            def rows_step(r, carry):
-                rows = pl.ds(pl.multiple_of(r * step_rows, step_rows), step_rows)
-                unit_of = lax.broadcasted_iota(jnp.int32, (1, keys), 1) >> 7
-                bias = jnp.where(rank_of(unit_of) < n, 0.0, LOW)
-                kk = buf[g, :, 0:HEAD]
-                vv = jnp.concatenate([buf[g, :, HEAD:], jnp.ones((keys, HEAD), BF)], axis=1)
-                sc = scores_of(q[rows, :], kk) + bias
-                old = m_ref[rows, :]
-                high = jnp.maximum(old, jnp.max(sc, axis=1, keepdims=True))
-                pr = jnp.exp2(sc - jnp.concatenate([high] * 8, axis=1)).astype(BF)
-                shrink = jnp.exp2(old - high)
-                m_ref[rows, :] = high
-                acc[rows, :] = acc[rows, :] * jnp.concatenate([shrink] * 2, axis=1) + dot(pr, vv)
-                return carry
-
-            lax.fori_loop(0, q.shape[0] // step_rows, rows_step, 0)
+            def score(r):
+                sc = scores_of(buf[g, :, 0:HEAD], r)
+                s_ref[r % 2] = jnp.concatenate(
+                    [
+                        sc[u * BLK : (u + 1) * BLK] + jnp.where(rank(u) < n, 0.0, LOW)
+                        for u in range(8)
+                    ],
+                    axis=0,
+                )
+
+            def soften(r):
+                at = slice(r * cols, (r + 1) * cols)
+                sc = s_ref[r % 2]
+                old = m_ref[0:1, at]
+                high = jnp.maximum(old, jnp.max(sc, axis=0, keepdims=True))
+                p_ref[r % 2] = jnp.exp2(sc - high).astype(BF)
+                x_ref[r % 2] = jnp.broadcast_to(jnp.exp2(old - high), (8, cols))
+                m_ref[:, at] = jnp.broadcast_to(high, (8, cols))
+
+            def collect(r):
+                at = slice(r * cols, (r + 1) * cols)
+                vt = jnp.concatenate(
+                    [buf[g, u * BLK : (u + 1) * BLK, HEAD:] for u in range(8)], axis=1
+                )
+                vt = jnp.concatenate([vt, ones_rows], axis=0)
+                acc[:, at] = acc[:, at] * x_ref[r % 2][0:1] + dot(vt, p_ref[r % 2])
+
+            for k in range(tiles + 2):
+                if k < tiles:
+                    score(k)
+                if k >= 2:
+                    collect(k - 2)
+                if 1 <= k <= tiles:
+                    soften(k - 1)
 
     def attend_a(g):
-        attend(buf_a, g, x * 2 + zlo + jnp.where(g < y, 1, 0), lambda u: u)
+        attend(g, x * 2 + zlo + jnp.where(g < y, 1, 0), lambda u: u)
 
     def attend_b(g):
         count = jnp.where(g < x, 8, jnp.where(g == x, zlo * 4 + y, 0))
-        attend(buf_b, g, count, lambda u: (u & 1) * 4 + (u >> 1))
+        attend(4 + g, count, lambda u: (u & 1) * 4 + (u >> 1))
 
     for s in sides:
         s.own_p.wait_recv()
@@ -281,10 +297,17 @@
     attend_b(side_b.i)
     relay(2)
     relay(3)
-    attend_a(side_a.im)
-    attend_a(side_a.ip)
-    attend_b(side_b.im)
-    attend_b(side_b.ip)
+
+    def both_a(k, carry):
+        attend_a(lax.rem(y + 3 + 2 * k, 4))
+        return carry
+
+    def both_b(k, carry):
+        attend_b(lax.rem(x + 3 + 2 * k, 4))
+        return carry
+
+    lax.fori_loop(0, 2, both_a, 0)
+    lax.fori_loop(0, 2, both_b, 0)
     for k in range(4):
         side_a.opp_p[k].wait_recv()
         side_a.opp_m[k].wait_recv()
@@ -295,9 +318,9 @@
     attend_b(side_b.io)
 
     for h in range(heads):
-        rows = slice(h * 256, (h + 1) * 256)
+        at = slice(h * 256, (h + 1) * 256)
         att[:, h * HEAD : (h + 1) * HEAD] = (
-            acc[rows, 0:HEAD] / acc[rows, HEAD : 2 * HEAD]
+            (acc[0:HEAD, at] / acc[HEAD : HEAD + 1, at]).T
         ).astype(BF)
 
     wcopies[3].wait()
@@ -395,10 +418,12 @@
             pltpu.VMEM((2, BLK, HEAD), F32),
             pltpu.VMEM((2, BLK, HEAD), F32),
             pltpu.VMEM((heads * 256, HEAD), BF),
-            pltpu.VMEM((4, 8 * BLK, 2 * HEAD), BF),
-            pltpu.VMEM((4, 8 * BLK, 2 * HEAD), BF),
-            pltpu.VMEM((heads * 256, HEAD), F32),
-            pltpu.VMEM((heads * 256, 2 * HEAD), F32),
+            pltpu.VMEM((8, 8 * BLK, 2 * HEAD), BF),
+            pltpu.VMEM((8, heads * 256), F32),
+            pltpu.VMEM((HEAD + 16, heads * 256), F32),
+            pltpu.VMEM((2, 8 * BLK, 512), F32),
+            pltpu.VMEM((2, 8 * BLK, 512), BF),
+            pltpu.VMEM((2, 8, 512), F32),
             pltpu.VMEM((256, qcols), BF),
             pltpu.VMEM((4, BLK, d), F32),
             pltpu.VMEM((4, BLK, d), F32),

time: 123 us -> 91.4 us (0.74)
  Pallas kernels: 112 us -> 80.9 us
    pallas_call x1, Pallas kernels: 112 us -> 80.9 us  [on_device(): pl.pallas_call(layer_kernel, name='layer', out_shape=jax.ShapeDtypeStruct...]
where the time goes in v2:
time: 91.4 us; the launch traced here: 91.2 us
  Pallas kernels  80.9 us (89%)
  between operations  3.82 us (4%)
  local copies, waits for them, and re-layouts  3.53 us (4%)
  other arithmetic  2.96 us (3%)
    pallas_call x1, Pallas kernels, on_device(): pl.pallas_call(layer_kernel, name='layer', out_shape=jax.ShapeDtypeStruct...  80.9 us
    reshape x1, local copies, waits for them, and re-layouts, on_device(): return result.transpose(1, 0, 2).reshape(piece, width)  1.88 us

profile of v2, /device:TPU:7, one launch (start us, length us, event | category | flops | bytes accessed | tf_op | source)
XLA Modules:
  0.0 91.2 jit_solution(8576222547805463238)
XLA Ops:
  0.0 0.7 broadcast_multiply_fusion
  0.7 0.1 add_convert_fusion
  0.7 0.6 fusion.1
  5.1 0.5 fusion
  5.7 0.8 pad_maximum_fusion.1
  6.5 1.1 %constant_dynamic-slice_fusion.1 = (bf16[1,128,1024]{2,1,0:T(8,128)(2,1)S(1)}, bf16[1,128,1024]{2,1,0:T(8,128)(2,1)S(1)}) fusion(bf16[16,128,1024]{2,1,0:T(8,128)(2,1)} %bitcast.9, s32[]{:T(128)S(6)} %select_n.6, s32[]{:T(128)S(6)} %select_n.7), kind=kLoop, calls=%fused_computation.9 | loop fusion | bytes 1048584 | tf_op jit(solution)/shard_map/dynamic_slice | solution.py:385
  7.6 0.8 pad_maximum_fusion.own
  8.4 80.9 %layer.1 = bf16[4,64,1024]{2,1,0:T(8,128)(2,1)} custom-call(bf16[2,128,1024]{2,1,0:T(8,128)(2,1)} %pad_maximum_fusion.own, f32[2,128,128]{2,1,0:T(8,128)} %get-tuple-element.14.cosf, f32[2,128,128]{2,1,0:T(8,128)} %get-tuple-element.15.sinf, f32[1,4096]{1,0:T(1,128)} %bitcast.10, f32[1,4096]{1,0:T(1,128)} %bitcast.11, bf16[4096,1024]{1,0:T(8,128)(2,1)} %wq_hbm.1, ...), custom_call_target="tpu_custom_call" | custom-call | tf_op jit(solution)/shard_map/layer/pallas_call | solution.py:401
  89.3 1.9 %copy.10 = bf16[4,8,8,1024]{3,2,0,1:T(8,128)(2,1)} copy(bf16[4,8,8,1024]{3,2,1,0:T(8,128)(2,1)} %bitcast.8) | data formatting | bytes 1048576 | tf_op jit(solution)/shard_map/reshape | solution.py:448
  (1 shorter events, 0.0 us)

commit v3 on v2

--- a/solution.py
+++ b/solution.py
@@ -23,9 +23,9 @@
 
 
 def layer_kernel(
-    own, cosf, sinf, gain, router, wq_hbm, wk_hbm, wv_hbm, wo_hbm,
+    sel, freq, gain, router, resid_hbm, wq_hbm, wk_hbm, wv_hbm, wo_hbm,
     out,
-    wq, wkv, wo, part, zsame, zother, rel_p, rel_m,
+    resid, own, cosf, sinf, wq, wkv, wo, part, zsame, zother, rel_p, rel_m,
     qacc, kvacc, ssq, gsum, q, buf, m_ref, acc, s_ref, p_ref, x_ref, att,
     prem, ploc, d_out, d_in, dl_out, dl_in, zs_out, zr_rel, zr_in,
     ssem, rsem, wsem,
@@ -57,12 +57,18 @@
         pltpu.make_async_copy(wv_hbm, wkv.at[:, HEAD : 2 * HEAD], wsem.at[2]),
         pltpu.make_async_copy(wo_hbm, wo, wsem.at[3]),
     ]
+    rcopy = pltpu.make_async_copy(resid_hbm, resid, wsem.at[4])
+    rcopy.start()
     for copy in wcopies:
         copy.start()
 
     barrier = pltpu.get_barrier_semaphore()
     for peer in (mate, up, down, right_x, left_x, right_y, left_y):
         pl.semaphore_signal(barrier, inc=1, device_id=peer, device_id_type=MESH)
+    rcopy.wait()
+    for b in range(2):
+        at = jnp.clip(sel[b] - c * resid.shape[0], 0, resid.shape[0] - 1)
+        own[b] = resid[at]
     pl.semaphore_wait(barrier, 7)
 
     made = []
@@ -87,6 +93,13 @@
         to_down[b].start()
         to_mate[b].start()
 
+    lane = lax.broadcasted_iota(jnp.int32, (BLK, HEAD), 1)
+    row = lax.broadcasted_iota(jnp.int32, (BLK, HEAD), 0)
+    for b in range(2):
+        angle = (row + sel[b] * BLK).astype(F32) * freq[...]
+        cosf[b] = jnp.cos(angle)
+        sine = jnp.sin(angle)
+        sinf[b] = jnp.where(lane < HEAD // 2, -sine, sine)
     ssq[...] = jnp.zeros_like(ssq)
     gsum[...] = jnp.zeros_like(gsum)
     src_own, src_mate = t, t + 1 - 2 * core
@@ -170,7 +183,7 @@
         s.pair_p = [copy_to(pair_at(base, i, k), pair_at(base, i, k), plus2) for k in s.order]
         s.pair_m = [copy_to(pair_at(base, i, k), pair_at(base, i, k), minus2) for k in s.order]
         im, ip = (i + 3) % 4, (i + 1) % 4
-        s.i, s.im, s.ip, s.io = i, im, ip, (i + 2) % 4
+        s.base, s.i, s.j, s.im, s.ip, s.io = base, i, j, im, ip, (i + 2) % 4
         s.opp_p = [copy_to(unit_at(base, im, k, 0), unit_at(base, im, k, 0), plus2) for k in s.order]
         s.opp_m = [copy_to(unit_at(base, ip, k, 1), unit_at(base, ip, k, 1), minus2) for k in s.order]
         return s
@@ -223,14 +236,24 @@
         m_ref[:, at] = jnp.broadcast_to(high, (8, cols))
         acc[:, at] = dot(v_own, pr)
 
-    def attend(g, n, rank):
-        @pl.when(n > 0)
+    def attend(pairs):
+        allowed = []
+        for base, i, j in pairs:
+            for k in range(2):
+                place = i * 8 + j if base else j * 8 + i
+                allowed.append(place + k * 4 < c)
+        some = allowed[0]
+        for flag in allowed[1:]:
+            some = jnp.logical_or(some, flag)
+
+        @pl.when(some)
         def _():
             def score(r):
-                sc = scores_of(buf[g, :, 0:HEAD], r)
+                ks = jnp.concatenate([pair_at(*pr)[:, 0:HEAD] for pr in pairs], axis=0)
+                sc = scores_of(ks, r)
                 s_ref[r % 2] = jnp.concatenate(
                     [
-                        sc[u * BLK : (u + 1) * BLK] + jnp.where(rank(u) < n, 0.0, LOW)
+                        sc[u * BLK : (u + 1) * BLK] + jnp.where(allowed[u], 0.0, LOW)
                         for u in range(8)
                     ],
                     axis=0,
@@ -248,7 +271,7 @@
             def collect(r):
                 at = slice(r * cols, (r + 1) * cols)
                 vt = jnp.concatenate(
-                    [buf[g, u * BLK : (u + 1) * BLK, HEAD:] for u in range(8)], axis=1
+                    [unit_at(*pr, k)[:, HEAD:] for pr in pairs for k in range(2)], axis=1
                 )
                 vt = jnp.concatenate([vt, ones_rows], axis=0)
                 acc[:, at] = acc[:, at] * x_ref[r % 2][0:1] + dot(vt, p_ref[r % 2])
@@ -261,12 +284,18 @@
                 if 1 <= k <= tiles:
                     soften(k - 1)
 
-    def attend_a(g):
-        attend(g, x * 2 + zlo + jnp.where(g < y, 1, 0), lambda u: u)
-
-    def attend_b(g):
-        count = jnp.where(g < x, 8, jnp.where(g == x, zlo * 4 + y, 0))
-        attend(4 + g, count, lambda u: (u & 1) * 4 + (u >> 1))
+    def attend_own(k0, k1):
+        attend([(s.base, s.i, s.order[k]) for s in sides for k in (k0, k1)])
+
+    def attend_near(step):
+        attend([(s.base, g, lax.rem(s.j + step, 4)) for s in sides for g in (s.im, s.ip)])
+
+    def attend_far(k0, k1):
+        for s in sides:
+            for k in (k0, k1):
+                s.opp_p[k].wait_recv()
+                s.opp_m[k].wait_recv()
+        attend([(s.base, s.io, s.order[k]) for s in sides for k in (k0, k1)])
 
     for s in sides:
         s.own_p.wait_recv()
@@ -278,6 +307,7 @@
         for k in (1, 2):
             s.pair_p[k].start()
             s.pair_m[k].start()
+    attend_own(0, 1)
     for s in sides:
         s.rel_p.wait_recv()
         s.rel_m.wait_recv()
@@ -292,30 +322,20 @@
             s.opp_m[k].start()
 
     relay(0)
-    attend_a(side_a.i)
+    attend_own(2, 3)
     relay(1)
-    attend_b(side_b.i)
+    attend_near(0)
     relay(2)
+    attend_near(3)
     relay(3)
 
-    def both_a(k, carry):
-        attend_a(lax.rem(y + 3 + 2 * k, 4))
+    def near_step(k, carry):
+        attend_near(k)
         return carry
 
-    def both_b(k, carry):
-        attend_b(lax.rem(x + 3 + 2 * k, 4))
-        return carry
-
-    lax.fori_loop(0, 2, both_a, 0)
-    lax.fori_loop(0, 2, both_b, 0)
-    for k in range(4):
-        side_a.opp_p[k].wait_recv()
-        side_a.opp_m[k].wait_recv()
-    attend_a(side_a.io)
-    for k in range(4):
-        side_b.opp_p[k].wait_recv()
-        side_b.opp_m[k].wait_recv()
-    attend_b(side_b.io)
+    lax.fori_loop(1, 3, near_step, 0)
+    attend_far(0, 1)
+    attend_far(2, 3)
 
     for h in range(heads):
         at = slice(h * 256, (h + 1) * 256)
@@ -369,7 +389,7 @@
         second_hop[j].wait_recv()
     for ref, s in ((own, src_own), (part, src_mate), (zsame, src_same), (zother, src_other)):
         total = ploc[s, mine, :] + zr_in[s].astype(F32)
-        out[s] = (ref[zhi, mine, :].astype(F32) + gate * total).astype(BF)
+        out[:, pl.ds(pl.multiple_of(s * d, d), d)] = (ref[zhi, mine, :].astype(F32) + gate * total).astype(BF)
 
     for copy in made:
         copy.wait_send()
@@ -379,19 +399,10 @@
     local_rows, d = resid.shape
     width = w_out.shape[1]
     count = local_rows // BLK
-    local_ids = sel_blocks - lax.axis_index("ctx") * count
-    blocks = resid.reshape(count, BLK, d)
-    own = jnp.concatenate(
-        [lax.dynamic_slice_in_dim(blocks, local_ids[b], 1, 0) for b in range(2)], axis=0
-    )
-    positions = sel_blocks[:, None] * BLK + jnp.arange(BLK, dtype=jnp.int32)[None, :]
     freqs = jnp.exp(
         jnp.arange(HEAD // 2, dtype=F32) * (-2.0 * math.log(rope_base) / HEAD)
     )
-    angles = positions.astype(F32)[:, :, None] * freqs[None, None, :]
-    cosine, sine = jnp.cos(angles), jnp.sin(angles)
-    cosf = jnp.concatenate([cosine, cosine], axis=2)
-    sinf = jnp.concatenate([-sine, sine], axis=2)
+    freqs = jnp.concatenate([freqs, freqs]).reshape(1, HEAD)
     qcols = w_query.shape[1]
     heads = qcols // HEAD
     vmem = pl.BlockSpec(memory_space=pltpu.VMEM)
@@ -401,10 +412,14 @@
     result = pl.pallas_call(
         layer_kernel,
         name="layer",
-        out_shape=jax.ShapeDtypeStruct((4, piece, d), BF),
-        in_specs=[vmem] * 5 + [anyspace] * 4,
+        out_shape=jax.ShapeDtypeStruct((piece, width), BF),
+        in_specs=[pl.BlockSpec(memory_space=pltpu.SMEM)] + [vmem] * 3 + [anyspace] * 5,
         out_specs=vmem,
         scratch_shapes=[
+            pltpu.VMEM((count, BLK, d), BF),
+            pltpu.VMEM((2, BLK, d), BF),
+            pltpu.VMEM((2, BLK, HEAD), F32),
+            pltpu.VMEM((2, BLK, HEAD), F32),
             pltpu.VMEM((width, qcols), BF),
             pltpu.VMEM((width, 2 * HEAD), BF),
             pltpu.VMEM((qcols, width), BF),
@@ -436,16 +451,16 @@
             pltpu.VMEM((4, piece, d), BF),
             pltpu.SemaphoreType.DMA((nsem,)),
             pltpu.SemaphoreType.DMA((nsem,)),
-            pltpu.SemaphoreType.DMA((4,)),
+            pltpu.SemaphoreType.DMA((5,)),
         ],
         compiler_params=pltpu.CompilerParams(
             collective_id=0, has_side_effects=True, vmem_limit_bytes=60 * 1024 * 1024
         ),
     )(
-        own, cosf, sinf, norm_gain.reshape(1, width), router_weight.reshape(1, width),
-        w_query, w_key, value_projection, w_out,
+        sel_blocks, freqs, norm_gain.reshape(1, width), router_weight.reshape(1, width),
+        resid.reshape(count, BLK, d), w_query, w_key, value_projection, w_out,
     )
-    return result.transpose(1, 0, 2).reshape(piece, width)
+    return result
 
 
 def solution(mesh):

time: 91.4 us -> 81.7 us (0.89)
  between operations: 3.82 us -> 0.01 us
  other arithmetic: 2.96 us -> 0.6 us
  Pallas kernels: 80.9 us -> 79.1 us
  local copies, waits for them, and re-layouts: 3.53 us -> 1.87 us
    reshape x1 -> x0, local copies, waits for them, and re-layouts: 1.88 us -> none  [on_device(): return result.transpose(1, 0, 2).reshape(piece, width)]
    unnamed x0 -> x1, local copies, waits for them, and re-layouts: none -> 1.87 us
    pallas_call x1, Pallas kernels: 80.9 us -> 79.1 us  [on_device(): pl.pallas_call(layer_kernel, name='layer', out_shape=jax.ShapeDtypeStruct...]
    concatenate x2 -> x0, other arithmetic: 1.68 us -> none  [the longest x1 0.84 us: on_device(): jnp.concatenate([lax.dynamic_slice_in_dim(blocks, local_ids[b], 1, 0) for...]
    dynamic_slice x1 -> x0, local copies, waits for them, and re-layouts: 1.06 us -> none  [on_device(): lax.dynamic_slice_in_dim(blocks, local_ids[b], 1, 0)]
where the time goes in v3:
time: 81.7 us; the launch traced here: 81.5 us
  Pallas kernels  79.1 us (97%)
  local copies, waits for them, and re-layouts  1.87 us (2%)
    pallas_call x1, Pallas kernels, on_device(): pl.pallas_call(layer_kernel, name='layer', out_shape=jax.ShapeDtypeStruct...  79.1 us
    unnamed x1, local copies, waits for them, and re-layouts  1.87 us

profile of v3, /device:TPU:7, one launch (start us, length us, event | category | flops | bytes accessed | tf_op | source)
XLA Modules:
  0.0 81.5 jit_solution(9375820505079654126)
XLA Ops:
  0.0 0.6 maximum_bitcast_fusion.freq
  0.6 79.1 %layer.1 = bf16[64,4096]{1,0:T(8,128)(2,1)} custom-call(s32[2]{0:T(128)} %sel.1, f32[1,128]{1,0:T(1,128)} %maximum_bitcast_fusion.freq, f32[1,4096]{1,0:T(1,128)} %bitcast.6, f32[1,4096]{1,0:T(1,128)} %bitcast.7, bf16[16,128,1024]{2,1,0:T(8,128)(2,1)} %bitcast.5, bf16[4096,1024]{1,0:T(8,128)(2,1)} %wq_hbm.1, bf16[4096,128]{1,0:T(8,128)(2,1)} %wk_hbm.1, ...), custom_call_target="tpu_custom_call" | custom-call | tf_op jit(solution)/shard_map/layer/pallas_call | solution.py:412
  79.7 1.9 %copy.10 = bf16[64,4096]{1,0:T(8,128)(2,1)} copy(bf16[64,4096]{1,0:T(8,128)(2,1)} %layer.1) | data formatting | bytes 1048576
  (1 shorter events, 0.0 us)

commit v4 on v3

--- a/solution.py
+++ b/solution.py
@@ -152,9 +152,6 @@
     def unit_at(base, i, j, k):
         return buf.at[base + i, pl.ds(pl.multiple_of((j * 2 + k) * BLK, BLK), BLK)]
 
-    def pair_at(base, i, j):
-        return buf.at[base + i, pl.ds(pl.multiple_of(j * 2 * BLK, 2 * BLK), 2 * BLK)]
-
     own_a = unit_at(0, y, x, zlo)
     own_b = unit_at(4, x, y, zlo)
     scale = math.log2(math.e) / math.sqrt(HEAD)
@@ -165,37 +162,53 @@
         unit[:, HEAD : 2 * HEAD] = kv[:, HEAD:].T.astype(BF)
 
     class Side:
-        pass
-
-    def side(base, i, j, plus1, minus1, plus2, minus2):
-        s = Side()
-        own_unit = unit_at(base, i, j, zlo)
-        s.to_z = copy_to(own_unit, own_unit, zpair)
-        z_unit = unit_at(base, i, j, 1 - zlo)
-        s.own_p = copy_to(own_unit, own_unit, plus1)
-        s.own_m = copy_to(own_unit, own_unit, minus1)
-        s.z_p = copy_to(z_unit, z_unit, plus1)
-        s.z_m = copy_to(z_unit, z_unit, minus1)
-        jm, jp = (j + 3) % 4, (j + 1) % 4
-        s.rel_p = copy_to(unit_at(base, i, jm, 0), unit_at(base, i, jm, 0), plus1)
-        s.rel_m = copy_to(unit_at(base, i, jp, 1), unit_at(base, i, jp, 1), minus1)
-        s.order = (j, jm, jp, (j + 2) % 4)
-        s.pair_p = [copy_to(pair_at(base, i, k), pair_at(base, i, k), plus2) for k in s.order]
-        s.pair_m = [copy_to(pair_at(base, i, k), pair_at(base, i, k), minus2) for k in s.order]
-        im, ip = (i + 3) % 4, (i + 1) % 4
-        s.base, s.i, s.j, s.im, s.ip, s.io = base, i, j, im, ip, (i + 2) % 4
-        s.opp_p = [copy_to(unit_at(base, im, k, 0), unit_at(base, im, k, 0), plus2) for k in s.order]
-        s.opp_m = [copy_to(unit_at(base, ip, k, 1), unit_at(base, ip, k, 1), minus2) for k in s.order]
-        return s
-
-    side_a = side(0, y, x, right_x, left_x, right_y, left_y)
-    side_b = side(4, x, y, right_y, left_y, right_x, left_x)
-    sides = (side_a, side_b)
+        def __init__(self, base, i, j, plus1, minus1, plus2, minus2):
+            self.base, self.i, self.j = base, i, j
+            first, second = (plus1, minus1), (plus2, minus2)
+            self.to_z = self.send(0, 0, 0, zpair)
+            self.own1 = [self.send(0, 0, 0, peer) for peer in first]
+            self.own2 = [self.send(0, 0, 0, peer) for peer in second]
+            self.z1 = [self.send(0, 0, 1, peer) for peer in first]
+            self.z2 = [self.send(0, 0, 1, peer) for peer in second]
+            self.half1 = [self.send(0, -1, 0, plus1), self.send(0, 1, 1, minus1)]
+            self.cross = {
+                (r, k): [self.send(0, r, k, peer) for peer in second]
+                for r in (-1, 1, 2)
+                for k in range(2)
+            }
+            self.far = {
+                (r, k): self.send(1 if k else -1, r, k, minus2 if k else plus2)
+                for r in (0, -1, 1, 2)
+                for k in range(2)
+            }
+
+        def place(self, di, dj, k):
+            plane = 1 - zlo if k else zlo
+            return lax.rem(self.i + di + 4, 4), lax.rem(self.j + dj + 4, 4), plane
+
+        def unit(self, di, dj, k):
+            return unit_at(self.base, *self.place(di, dj, k))
+
+        def send(self, di, dj, k, peer):
+            return copy_to(self.unit(di, dj, k), self.unit(di, dj, k), peer)
+
+        def allowed(self, di, dj, k):
+            i, j, plane = self.place(di, dj, k)
+            return (i * 8 + j if self.base else j * 8 + i) + plane * 4 < c
+
+    sides = (
+        Side(0, y, x, right_x, left_x, right_y, left_y),
+        Side(4, x, y, right_y, left_y, right_x, left_x),
+    )
+
+    def start(*groups):
+        for group in groups:
+            for copy in group:
+                copy.start()
 
     for s in sides:
         s.to_z.start()
-        s.own_p.start()
-        s.own_m.start()
+        start(s.own1, s.own2)
 
     for b in range(2):
         inv = lax.rsqrt(ssq[b][:, 0:1] * (1.0 / width) + norm_eps)
@@ -204,13 +217,6 @@
             q[h * 256 + b * BLK : h * 256 + (b + 1) * BLK, :] = (
                 rotated(qh, b) * scale
             ).astype(BF)
-
-    for s in sides:
-        s.to_z.wait_recv()
-        s.z_p.start()
-        s.z_m.start()
-        s.pair_p[0].start()
-        s.pair_m[0].start()
 
     cols = 512
     tiles = heads * 256 // cols
@@ -236,12 +242,9 @@
         m_ref[:, at] = jnp.broadcast_to(high, (8, cols))
         acc[:, at] = dot(v_own, pr)
 
-    def attend(pairs):
-        allowed = []
-        for base, i, j in pairs:
-            for k in range(2):
-                place = i * 8 + j if base else j * 8 + i
-                allowed.append(place + k * 4 < c)
+    def attend(places):
+        units = [(s, p) for s in sides for p in places]
+        allowed = [s.allowed(*p) for s, p in units]
         some = allowed[0]
         for flag in allowed[1:]:
             some = jnp.logical_or(some, flag)
@@ -249,7 +252,7 @@
         @pl.when(some)
         def _():
             def score(r):
-                ks = jnp.concatenate([pair_at(*pr)[:, 0:HEAD] for pr in pairs], axis=0)
+                ks = jnp.concatenate([s.unit(*p)[:, 0:HEAD] for s, p in units], axis=0)
                 sc = scores_of(ks, r)
                 s_ref[r % 2] = jnp.concatenate(
                     [
@@ -271,7 +274,7 @@
             def collect(r):
                 at = slice(r * cols, (r + 1) * cols)
                 vt = jnp.concatenate(
-                    [unit_at(*pr, k)[:, HEAD:] for pr in pairs for k in range(2)], axis=1
+                    [s.unit(*p)[:, HEAD:] for s, p in units], axis=1
                 )
                 vt = jnp.concatenate([vt, ones_rows], axis=0)
                 acc[:, at] = acc[:, at] * x_ref[r % 2][0:1] + dot(vt, p_ref[r % 2])
@@ -284,58 +287,58 @@
                 if 1 <= k <= tiles:
                     soften(k - 1)
 
-    def attend_own(k0, k1):
-        attend([(s.base, s.i, s.order[k]) for s in sides for k in (k0, k1)])
-
-    def attend_near(step):
-        attend([(s.base, g, lax.rem(s.j + step, 4)) for s in sides for g in (s.im, s.ip)])
-
-    def attend_far(k0, k1):
+    for s in sides:
+        s.to_z.wait_recv()
+        start(s.z1, s.z2)
+    for s in sides:
+        s.own1[0].wait_recv()
+        s.half1[0].start()
+        start(s.cross[-1, 0])
+        s.own1[1].wait_recv()
+        start(s.cross[1, 0])
+        s.own2[0].wait_recv()
+        s.far[0, 0].start()
+        s.own2[1].wait_recv()
+    attend([(0, -1, 0), (0, 1, 0), (-1, 0, 0), (1, 0, 0)])
+    for s in sides:
+        s.z1[0].wait_recv()
+        start(s.cross[-1, 1])
+        s.z1[1].wait_recv()
+        s.half1[1].start()
+        start(s.cross[1, 1])
+        s.z2[0].wait_recv()
+        s.z2[1].wait_recv()
+        s.far[0, 1].start()
+    attend([(0, -1, 1), (0, 1, 1), (-1, 0, 1), (1, 0, 1)])
+
+    def relay(r, k):
         for s in sides:
-            for k in (k0, k1):
-                s.opp_p[k].wait_recv()
-                s.opp_m[k].wait_recv()
-        attend([(s.base, s.io, s.order[k]) for s in sides for k in (k0, k1)])
-
-    for s in sides:
-        s.own_p.wait_recv()
-        s.z_p.wait_recv()
-        s.rel_p.start()
-        s.own_m.wait_recv()
-        s.z_m.wait_recv()
-        s.rel_m.start()
-        for k in (1, 2):
-            s.pair_p[k].start()
-            s.pair_m[k].start()
-    attend_own(0, 1)
-    for s in sides:
-        s.rel_p.wait_recv()
-        s.rel_m.wait_recv()
-        s.pair_p[3].start()
-        s.pair_m[3].start()
-
-    def relay(k):
+            for copy in s.cross[r, k]:
+                copy.wait_recv()
+            s.far[r, k].start()
+
+    for s in sides:
+        s.half1[0].wait_recv()
+        start(s.cross[2, 0])
+    relay(-1, 0)
+    relay(1, 0)
+    attend([(di, dj, 0) for di in (-1, 1) for dj in (-1, 1)])
+    for s in sides:
+        s.half1[1].wait_recv()
+        start(s.cross[2, 1])
+    attend([(0, 0, 0), (0, 0, 1), (0, 2, 0), (0, 2, 1)])
+    relay(-1, 1)
+    relay(1, 1)
+    attend([(di, dj, 1) for di in (-1, 1) for dj in (-1, 1)])
+    relay(2, 0)
+    relay(2, 1)
+    attend([(di, 2, k) for di in (-1, 1) for k in range(2)])
+    for rs in ((0, -1), (1, 2)):
         for s in sides:
-            s.pair_p[k].wait_recv()
-            s.opp_p[k].start()
-            s.pair_m[k].wait_recv()
-            s.opp_m[k].start()
-
-    relay(0)
-    attend_own(2, 3)
-    relay(1)
-    attend_near(0)
-    relay(2)
-    attend_near(3)
-    relay(3)
-
-    def near_step(k, carry):
-        attend_near(k)
-        return carry
-
-    lax.fori_loop(1, 3, near_step, 0)
-    attend_far(0, 1)
-    attend_far(2, 3)
+            for r in rs:
+                s.far[r, 0].wait_recv()
+                s.far[r, 1].wait_recv()
+        attend([(2, r, k) for r in rs for k in range(2)])
 
     for h in range(heads):
         at = slice(h * 256, (h + 1) * 256)
@@ -408,7 +411,7 @@
     vmem = pl.BlockSpec(memory_space=pltpu.VMEM)
     anyspace = pl.BlockSpec(memory_space=pl.ANY)
     piece = BLK // 2
-    nsem = 74
+    nsem = 90
     result = pl.pallas_call(
         layer_kernel,
         name="layer",

time: 81.7 us -> 76.3 us (0.934)
  Pallas kernels: 79.1 us -> 73.6 us
    pallas_call x1, Pallas kernels: 79.1 us -> 73.6 us  [on_device(): pl.pallas_call(layer_kernel, name='layer', out_shape=jax.ShapeDtypeStruct...]
where the time goes in v4:
time: 76.3 us; the launch traced here: 76 us
  Pallas kernels  73.6 us (96%)
  local copies, waits for them, and re-layouts  1.87 us (2%)
    pallas_call x1, Pallas kernels, on_device(): pl.pallas_call(layer_kernel, name='layer', out_shape=jax.ShapeDtypeStruct...  73.6 us
    unnamed x1, local copies, waits for them, and re-layouts  1.87 us

profile of v4, /device:TPU:7, one launch (start us, length us, event | category | flops | bytes accessed | tf_op | source)
XLA Modules:
  0.0 76.0 jit_solution(14710652240811093067)
XLA Ops:
  0.0 0.6 maximum_bitcast_fusion.freq
  0.6 73.6 %layer.1 = bf16[64,4096]{1,0:T(8,128)(2,1)} custom-call(s32[2]{0:T(128)} %sel.1, f32[1,128]{1,0:T(1,128)} %maximum_bitcast_fusion.freq, f32[1,4096]{1,0:T(1,128)} %bitcast.6, f32[1,4096]{1,0:T(1,128)} %bitcast.7, bf16[16,128,1024]{2,1,0:T(8,128)(2,1)} %bitcast.5, bf16[4096,1024]{1,0:T(8,128)(2,1)} %wq_hbm.1, bf16[4096,128]{1,0:T(8,128)(2,1)} %wk_hbm.1, ...), custom_call_target="tpu_custom_call" | custom-call | tf_op jit(solution)/shard_map/layer/pallas_call | solution.py:415
  74.2 1.9 %copy.10 = bf16[64,4096]{1,0:T(8,128)(2,1)} copy(bf16[64,4096]{1,0:T(8,128)(2,1)} %layer.1) | data formatting | bytes 1048576
  (1 shorter events, 0.0 us)

commit v5 on v4

--- a/solution.py
+++ b/solution.py
@@ -93,59 +93,6 @@
         to_down[b].start()
         to_mate[b].start()
 
-    lane = lax.broadcasted_iota(jnp.int32, (BLK, HEAD), 1)
-    row = lax.broadcasted_iota(jnp.int32, (BLK, HEAD), 0)
-    for b in range(2):
-        angle = (row + sel[b] * BLK).astype(F32) * freq[...]
-        cosf[b] = jnp.cos(angle)
-        sine = jnp.sin(angle)
-        sinf[b] = jnp.where(lane < HEAD // 2, -sine, sine)
-    ssq[...] = jnp.zeros_like(ssq)
-    gsum[...] = jnp.zeros_like(gsum)
-    src_own, src_mate = t, t + 1 - 2 * core
-    src_same = (t + 2) % 4
-    src_other = (src_mate + 2) % 4
-
-    def project(ref, b, s, first):
-        at = pl.multiple_of(s * d, d)
-        rows = pl.ds(at, d)
-        ch = ref[b].astype(F32)
-        ssq[b] += jnp.broadcast_to(jnp.sum(ch * ch, axis=1, keepdims=True), (BLK, HEAD))
-        gsum[b] += jnp.broadcast_to(
-            jnp.sum(ch * router[:, rows], axis=1, keepdims=True), (BLK, HEAD)
-        )
-        cg = (ch * gain[:, rows]).astype(BF)
-        pq = dot(cg, wq[rows, :])
-        pkv = dot(cg, wkv[rows, :])
-        if first:
-            qacc[b] = pq
-            kvacc[b] = pkv
-        else:
-            qacc[b] += pq
-            kvacc[b] += pkv
-
-    for copy in wcopies[:3]:
-        copy.wait()
-    for b in range(2):
-        project(own, b, src_own, True)
-    for b in range(2):
-        to_up[b].wait_recv()
-        fwd_up[b].start()
-        to_down[b].wait_recv()
-        fwd_down[b].start()
-        if b == 0:
-            for bb in range(2):
-                to_mate[bb].wait_recv()
-                project(part, bb, src_mate, False)
-    for b in range(2):
-        fwd_up[b].wait_recv()
-        fwd_down[b].wait_recv()
-        fwd_mate[b].start()
-        project(zsame, b, src_same, False)
-    for b in range(2):
-        fwd_mate[b].wait_recv()
-        project(zother, b, src_other, False)
-
     def rotated(v, b):
         return v * cosf[b] + pltpu.roll(v, HEAD // 2, 1) * sinf[b]
 
@@ -155,11 +102,20 @@
     own_a = unit_at(0, y, x, zlo)
     own_b = unit_at(4, x, y, zlo)
     scale = math.log2(math.e) / math.sqrt(HEAD)
-    for b, unit in ((0, own_a), (1, own_b)):
-        inv = lax.rsqrt(ssq[b][:, 0:1] * (1.0 / width) + norm_eps)
-        kv = kvacc[b] * inv
+    span = heads * BLK
+
+    def finish_keys(b):
+        unit = own_b if b else own_a
+        kv = kvacc[b] * lax.rsqrt(ssq[b][:, 0:1] * (1.0 / width) + norm_eps)
         unit[:, 0:HEAD] = rotated(kv[:, 0:HEAD], b).astype(BF)
         unit[:, HEAD : 2 * HEAD] = kv[:, HEAD:].T.astype(BF)
+
+    def finish_queries(b):
+        inv = lax.rsqrt(ssq[b][:, 0:1] * (1.0 / width) + norm_eps)
+        for h in range(heads):
+            qh = qacc[b][:, h * HEAD : (h + 1) * HEAD] * inv
+            at = b * span + h * BLK
+            q[at : at + BLK, :] = (rotated(qh, b) * scale).astype(BF)
 
     class Side:
         def __init__(self, base, i, j, plus1, minus1, plus2, minus2):
@@ -206,85 +162,141 @@
             for copy in group:
                 copy.start()
 
-    for s in sides:
-        s.to_z.start()
-        start(s.own1, s.own2)
-
+    lane = lax.broadcasted_iota(jnp.int32, (BLK, HEAD), 1)
+    row = lax.broadcasted_iota(jnp.int32, (BLK, HEAD), 0)
     for b in range(2):
-        inv = lax.rsqrt(ssq[b][:, 0:1] * (1.0 / width) + norm_eps)
-        for h in range(heads):
-            qh = qacc[b][:, h * HEAD : (h + 1) * HEAD] * inv
-            q[h * 256 + b * BLK : h * 256 + (b + 1) * BLK, :] = (
-                rotated(qh, b) * scale
-            ).astype(BF)
+        angle = (row + sel[b] * BLK).astype(F32) * freq[...]
+        cosf[b] = jnp.cos(angle)
+        sine = jnp.sin(angle)
+        sinf[b] = jnp.where(lane < HEAD // 2, -sine, sine)
+    ssq[...] = jnp.zeros_like(ssq)
+    gsum[...] = jnp.zeros_like(gsum)
+    src_own, src_mate = t, t + 1 - 2 * core
+    src_same = (t + 2) % 4
+    src_other = (src_mate + 2) % 4
+
+    def project(ref, b, s, first=False):
+        rows = pl.ds(pl.multiple_of(s * d, d), d)
+        ch = ref[b].astype(F32)
+        ssq[b] += jnp.broadcast_to(jnp.sum(ch * ch, axis=1, keepdims=True), (BLK, HEAD))
+        gsum[b] += jnp.broadcast_to(
+            jnp.sum(ch * router[:, rows], axis=1, keepdims=True), (BLK, HEAD)
+        )
+        cg = (ch * gain[:, rows]).astype(BF)
+
+        def into(total, weight):
+            part_sum = dot(cg, weight[rows, :])
+            if first:
+                total[b] = part_sum
+            else:
+                total[b] += part_sum
+
+        into(kvacc, wkv)
+        return lambda: into(qacc, wq)
+
+    def relay_features(b):
+        to_up[b].wait_recv()
+        fwd_up[b].start()
+        to_down[b].wait_recv()
+        fwd_down[b].start()
+
+    relay_features(0)
+    for copy in wcopies[:3]:
+        copy.wait()
+    for b in range(2):
+        project(own, b, src_own, True)()
+    relay_features(1)
+    for b in range(2):
+        to_mate[b].wait_recv()
+        project(part, b, src_mate)()
+    for b in range(2):
+        fwd_up[b].wait_recv()
+        fwd_down[b].wait_recv()
+        fwd_mate[b].start()
+        project(zsame, b, src_same)()
+        fwd_mate[b].wait_recv()
+        rest = project(zother, b, src_other)
+        finish_keys(b)
+        sides[b].to_z.start()
+        start(sides[b].own1, sides[b].own2)
+        rest()
+        finish_queries(b)
 
     cols = 512
-    tiles = heads * 256 // cols
+    tiles = span // cols
     ones_rows = jnp.ones((16, 8 * BLK), BF)
 
-    def scores_of(ks, r):
+    def scores_of(ks, at):
         return lax.dot_general(
-            ks, q[r * cols : (r + 1) * cols, :], (((1,), (1,)), ((), ())),
-            preferred_element_type=F32,
+            ks, q[at, :], (((1,), (1,)), ((), ())), preferred_element_type=F32
         )
 
     keys_own = jnp.concatenate([own_a[:, 0:HEAD], own_b[:, 0:HEAD]], axis=0)
     v_own = jnp.concatenate([own_a[:, HEAD:], own_b[:, HEAD:]], axis=1)
     v_own = jnp.concatenate([v_own, ones_rows[:, 0 : 2 * BLK]], axis=0)
     key_at = lax.broadcasted_iota(jnp.int32, (256, cols), 0)
-    query_at = lax.broadcasted_iota(jnp.int32, (256, cols), 1) & 255
-    upper = key_at <= query_at
-    for r in range(tiles):
+    query_at = lax.broadcasted_iota(jnp.int32, (256, cols), 1) & (BLK - 1)
+    for r in range(2 * tiles):
         at = slice(r * cols, (r + 1) * cols)
-        sc = jnp.where(upper, scores_of(keys_own, r), LOW)
+        seen = key_at <= query_at + (r // tiles) * BLK
+        sc = jnp.where(seen, scores_of(keys_own, at), LOW)
         high = jnp.max(sc, axis=0, keepdims=True)
-        pr = jnp.where(upper, jnp.exp2(sc - high), 0.0).astype(BF)
+        pr = jnp.where(seen, jnp.exp2(sc - high), 0.0).astype(BF)
         m_ref[:, at] = jnp.broadcast_to(high, (8, cols))
         acc[:, at] = dot(v_own, pr)
 
-    def attend(places):
-        units = [(s, p) for s in sides for p in places]
-        allowed = [s.allowed(*p) for s, p in units]
-        some = allowed[0]
-        for flag in allowed[1:]:
-            some = jnp.logical_or(some, flag)
+    def attend(groups, block=None):
+        units = [[(s, p) for s in sides for p in places] for places in groups]
+        allowed = [[s.allowed(*p) for s, p in group] for group in units]
+        some = allowed[0][0]
+        for flags in allowed:
+            for flag in flags:
+                some = jnp.logical_or(some, flag)
+        if block is None:
+            spots = [slice(r * cols, (r + 1) * cols) for r in range(2 * tiles)]
+        else:
+            spots = [
+                pl.ds(pl.multiple_of(block * span + r * cols, cols), cols)
+                for r in range(tiles)
+            ]
+        steps = [(g, at) for g in range(len(groups)) for at in spots]
 
         @pl.when(some)
         def _():
-            def score(r):
-                ks = jnp.concatenate([s.unit(*p)[:, 0:HEAD] for s, p in units], axis=0)
-                sc = scores_of(ks, r)
-                s_ref[r % 2] = jnp.concatenate(
+            def score(k):
+                g, at = steps[k]
+                ks = jnp.concatenate([s.unit(*p)[:, 0:HEAD] for s, p in units[g]], axis=0)
+                sc = scores_of(ks, at)
+                s_ref[k % 2] = jnp.concatenate(
                     [
-                        sc[u * BLK : (u + 1) * BLK] + jnp.where(allowed[u], 0.0, LOW)
+                        sc[u * BLK : (u + 1) * BLK] + jnp.where(allowed[g][u], 0.0, LOW)
                         for u in range(8)
                     ],
                     axis=0,
                 )
 
-            def soften(r):
-                at = slice(r * cols, (r + 1) * cols)
-                sc = s_ref[r % 2]
+            def soften(k):
+                at = steps[k][1]
+                sc = s_ref[k % 2]
                 old = m_ref[0:1, at]
                 high = jnp.maximum(old, jnp.max(sc, axis=0, keepdims=True))
-                p_ref[r % 2] = jnp.exp2(sc - high).astype(BF)
-                x_ref[r % 2] = jnp.broadcast_to(jnp.exp2(old - high), (8, cols))
+                p_ref[k % 2] = jnp.exp2(sc - high).astype(BF)
+                x_ref[k % 2] = jnp.broadcast_to(jnp.exp2(old - high), (8, cols))
                 m_ref[:, at] = jnp.broadcast_to(high, (8, cols))
 
-            def collect(r):
-                at = slice(r * cols, (r + 1) * cols)
-                vt = jnp.concatenate(
-                    [s.unit(*p)[:, HEAD:] for s, p in units], axis=1
-                )
+            def collect(k):
+                g, at = steps[k]
+                vt = jnp.concatenate([s.unit(*p)[:, HEAD:] for s, p in units[g]], axis=1)
                 vt = jnp.concatenate([vt, ones_rows], axis=0)
-                acc[:, at] = acc[:, at] * x_ref[r % 2][0:1] + dot(vt, p_ref[r % 2])
-
-            for k in range(tiles + 2):
-                if k < tiles:
+                acc[:, at] = acc[:, at] * x_ref[k % 2][0:1] + dot(vt, p_ref[k % 2])
+
+            count = len(steps)
+            for k in range(count + 2):
+                if k < count:
                     score(k)
                 if k >= 2:
                     collect(k - 2)
-                if 1 <= k <= tiles:
+                if 1 <= k <= count:
                     soften(k - 1)
 
     for s in sides:
@@ -299,7 +311,7 @@
         s.own2[0].wait_recv()
         s.far[0, 0].start()
         s.own2[1].wait_recv()
-    attend([(0, -1, 0), (0, 1, 0), (-1, 0, 0), (1, 0, 0)])
+    attend([[(0, -1, 0), (0, 1, 0), (-1, 0, 0), (1, 0, 0)]])
     for s in sides:
         s.z1[0].wait_recv()
         start(s.cross[-1, 1])
@@ -309,7 +321,7 @@
         s.z2[0].wait_recv()
         s.z2[1].wait_recv()
         s.far[0, 1].start()
-    attend([(0, -1, 1), (0, 1, 1), (-1, 0, 1), (1, 0, 1)])
+    attend([[(0, -1, 1), (0, 1, 1), (-1, 0, 1), (1, 0, 1)]])
 
     def relay(r, k):
         for s in sides:
@@ -322,29 +334,39 @@
         start(s.cross[2, 0])
     relay(-1, 0)
     relay(1, 0)
-    attend([(di, dj, 0) for di in (-1, 1) for dj in (-1, 1)])
+    attend([[(di, dj, 0) for di in (-1, 1) for dj in (-1, 1)]])
     for s in sides:
         s.half1[1].wait_recv()
         start(s.cross[2, 1])
-    attend([(0, 0, 0), (0, 0, 1), (0, 2, 0), (0, 2, 1)])
+    attend([[(0, 0, 0), (0, 0, 1), (0, 2, 0), (0, 2, 1)]])
     relay(-1, 1)
     relay(1, 1)
-    attend([(di, dj, 1) for di in (-1, 1) for dj in (-1, 1)])
+    last_groups = [
+        [(di, dj, 1) for di in (-1, 1) for dj in (-1, 1)],
+        [(di, 2, k) for di in (-1, 1) for k in range(2)],
+        [(2, r, k) for r in (0, -1) for k in range(2)],
+        [(2, r, k) for r in (1, 2) for k in range(2)],
+    ]
+    attend(last_groups[0:1], 1 - zhi)
     relay(2, 0)
     relay(2, 1)
-    attend([(di, 2, k) for di in (-1, 1) for k in range(2)])
-    for rs in ((0, -1), (1, 2)):
+    attend(last_groups[1:2], 1 - zhi)
+    for group, rs in ((2, (0, -1)), (3, (1, 2))):
         for s in sides:
             for r in rs:
                 s.far[r, 0].wait_recv()
                 s.far[r, 1].wait_recv()
-        attend([(2, r, k) for r in rs for k in range(2)])
-
-    for h in range(heads):
-        at = slice(h * 256, (h + 1) * 256)
-        att[:, h * HEAD : (h + 1) * HEAD] = (
-            (acc[0:HEAD, at] / acc[HEAD : HEAD + 1, at]).T
-        ).astype(BF)
+        attend(last_groups[group : group + 1], 1 - zhi)
+
+    def finish_attended(block):
+        rows = pl.ds(pl.multiple_of(block * BLK, BLK), BLK)
+        for h in range(heads):
+            at = pl.ds(pl.multiple_of(block * span + h * BLK, BLK), BLK)
+            att[rows, h * HEAD : (h + 1) * HEAD] = (
+                (acc[0:HEAD, at] / acc[HEAD : HEAD + 1, at]).T
+            ).astype(BF)
+
+    finish_attended(1 - zhi)
 
     wcopies[3].wait()
     piece = BLK // 2
@@ -376,13 +398,16 @@
             pass_on(last)
         last = j
     pass_on(last)
-    for k, j in enumerate(order):
+    for k in range(2):
+        attend(last_groups[2 * k : 2 * k + 2], zhi)
+        for j in order[2 * k : 2 * k + 2]:
+            first_hop[j].wait_recv()
+            second_hop[j].start()
+    finish_attended(zhi)
+    for j in order:
         ploc[j] = dot(att[near_rows, :], wo[:, j * d : (j + 1) * d])
         dl_out[j] = ploc[j, other, :].astype(BF)
         near_mate[j].start()
-    for j in order:
-        first_hop[j].wait_recv()
-        second_hop[j].start()
     for j in order:
         near_mate[j].wait_recv()
         ploc[j, mine, :] += dl_in[j].astype(F32)

time: 76.3 us -> 70.7 us (0.927)
  Pallas kernels: 73.6 us -> 68 us
    pallas_call x1, Pallas kernels: 73.6 us -> 68 us  [on_device(): pl.pallas_call(layer_kernel, name='layer', out_shape=jax.ShapeDtypeStruct...]
where the time goes in v5:
time: 70.7 us; the launch traced here: 70.5 us
  Pallas kernels  68 us (96%)
  local copies, waits for them, and re-layouts  1.87 us (3%)
    pallas_call x1, Pallas kernels, on_device(): pl.pallas_call(layer_kernel, name='layer', out_shape=jax.ShapeDtypeStruct...  68 us
    unnamed x1, local copies, waits for them, and re-layouts  1.87 us

profile of v5, /device:TPU:7, one launch (start us, length us, event | category | flops | bytes accessed | tf_op | source)
XLA Modules:
  0.0 70.5 jit_solution(5904762795652018008)
XLA Ops:
  0.0 0.6 maximum_bitcast_fusion.freq
  0.6 68.0 %layer.1 = bf16[64,4096]{1,0:T(8,128)(2,1)} custom-call(s32[2]{0:T(128)} %sel.1, f32[1,128]{1,0:T(1,128)} %maximum_bitcast_fusion.freq, f32[1,4096]{1,0:T(1,128)} %bitcast.6, f32[1,4096]{1,0:T(1,128)} %bitcast.7, bf16[16,128,1024]{2,1,0:T(8,128)(2,1)} %bitcast.5, bf16[4096,1024]{1,0:T(8,128)(2,1)} %wq_hbm.1, bf16[4096,128]{1,0:T(8,128)(2,1)} %wk_hbm.1, ...), custom_call_target="tpu_custom_call" | custom-call | tf_op jit(solution)/shard_map/layer/pallas_call | solution.py:440
  68.6 1.9 %copy.10 = bf16[64,4096]{1,0:T(8,128)(2,1)} copy(bf16[64,4096]{1,0:T(8,128)(2,1)} %layer.1) | data formatting | bytes 1048576
  (1 shorter events, 0.0 us)

commit v6 on v5

--- a/solution.py
+++ b/solution.py
@@ -2,6 +2,7 @@
 
 import jax
 import jax.numpy as jnp
+import numpy as np
 from jax import lax
 from jax.experimental import pallas as pl
 from jax.experimental.pallas import tpu as pltpu
@@ -23,9 +24,9 @@
 
 
 def layer_kernel(
-    sel, freq, gain, router, resid_hbm, wq_hbm, wk_hbm, wv_hbm, wo_hbm,
-    out,
-    resid, own, cosf, sinf, wq, wkv, wo, part, zsame, zother, rel_p, rel_m,
+    sel, freq_hbm, gain_hbm, router_hbm, resid_hbm, wq_hbm, wk_hbm, wv_hbm, wo_hbm,
+    out_hbm,
+    freq, gain, router, out, resid, own, cosf, sinf, wq, wkv, wo, part, zsame, zother, rel_p, rel_m,
     qacc, kvacc, ssq, gsum, q, buf, m_ref, acc, s_ref, p_ref, x_ref, att,
     prem, ploc, d_out, d_in, dl_out, dl_in, zs_out, zr_rel, zr_in,
     ssem, rsem, wsem,
@@ -58,13 +59,16 @@
         pltpu.make_async_copy(wo_hbm, wo, wsem.at[3]),
     ]
     rcopy = pltpu.make_async_copy(resid_hbm, resid, wsem.at[4])
-    rcopy.start()
-    for copy in wcopies:
-        copy.start()
-
+    small = [
+        pltpu.make_async_copy(freq_hbm, freq, wsem.at[5]),
+        pltpu.make_async_copy(gain_hbm, gain, wsem.at[6]),
+        pltpu.make_async_copy(router_hbm, router, wsem.at[7]),
+    ]
     barrier = pltpu.get_barrier_semaphore()
     for peer in (mate, up, down, right_x, left_x, right_y, left_y):
         pl.semaphore_signal(barrier, inc=1, device_id=peer, device_id_type=MESH)
+    for copy in (rcopy, *small, *wcopies):
+        copy.start()
     rcopy.wait()
     for b in range(2):
         at = jnp.clip(sel[b] - c * resid.shape[0], 0, resid.shape[0] - 1)
@@ -162,6 +166,8 @@
             for copy in group:
                 copy.start()
 
+    for copy in small:
+        copy.wait()
     lane = lax.broadcasted_iota(jnp.int32, (BLK, HEAD), 1)
     row = lax.broadcasted_iota(jnp.int32, (BLK, HEAD), 0)
     for b in range(2):
@@ -410,15 +416,27 @@
         near_mate[j].start()
     for j in order:
         near_mate[j].wait_recv()
-        ploc[j, mine, :] += dl_in[j].astype(F32)
 
     gate = 1.0 / (1.0 + jnp.exp(-gsum[zhi, mine, 0:1]))
+    for ref, s in ((own, src_own), (part, src_mate), (zsame, src_same), (zother, src_other)):
+        ploc[s, mine, :] = ref[zhi, mine, :].astype(F32) + gate * (
+            ploc[s, mine, :] + dl_in[s].astype(F32)
+        )
+    outs = [
+        pltpu.make_async_copy(
+            out.at[:, j * d : (j + 1) * d], out_hbm.at[:, j * d : (j + 1) * d], wsem.at[8 + j]
+        )
+        for j in range(4)
+    ]
     for j in order:
         second_hop[j].wait_recv()
-    for ref, s in ((own, src_own), (part, src_mate), (zsame, src_same), (zother, src_other)):
-        total = ploc[s, mine, :] + zr_in[s].astype(F32)
-        out[:, pl.ds(pl.multiple_of(s * d, d), d)] = (ref[zhi, mine, :].astype(F32) + gate * total).astype(BF)
-
+        out[:, j * d : (j + 1) * d] = (
+            ploc[j, mine, :] + gate * zr_in[j].astype(F32)
+        ).astype(BF)
+        outs[j].start()
+
+    for copy in outs:
+        copy.wait()
     for copy in made:
         copy.wait_send()
 
@@ -427,23 +445,26 @@
     local_rows, d = resid.shape
     width = w_out.shape[1]
     count = local_rows // BLK
-    freqs = jnp.exp(
-        jnp.arange(HEAD // 2, dtype=F32) * (-2.0 * math.log(rope_base) / HEAD)
+    powers = np.arange(HEAD // 2, dtype=np.float32) * np.float32(
+        -2.0 * math.log(rope_base) / HEAD
     )
-    freqs = jnp.concatenate([freqs, freqs]).reshape(1, HEAD)
+    freqs = jnp.asarray(np.tile(np.exp(powers), 2).reshape(1, HEAD), F32)
     qcols = w_query.shape[1]
     heads = qcols // HEAD
-    vmem = pl.BlockSpec(memory_space=pltpu.VMEM)
-    anyspace = pl.BlockSpec(memory_space=pl.ANY)
+    anyspace = pl.BlockSpec(memory_space=pltpu.HBM)
     piece = BLK // 2
     nsem = 90
     result = pl.pallas_call(
         layer_kernel,
         name="layer",
         out_shape=jax.ShapeDtypeStruct((piece, width), BF),
-        in_specs=[pl.BlockSpec(memory_space=pltpu.SMEM)] + [vmem] * 3 + [anyspace] * 5,
-        out_specs=vmem,
+        in_specs=[pl.BlockSpec(memory_space=pltpu.SMEM)] + [anyspace] * 8,
+        out_specs=anyspace,
         scratch_shapes=[
+            pltpu.VMEM((1, HEAD), F32),
+            pltpu.VMEM((1, width), F32),
+            pltpu.VMEM((1, width), F32),
+            pltpu.VMEM((piece, width), BF),
             pltpu.VMEM((count, BLK, d), BF),
             pltpu.VMEM((2, BLK, d), BF),
             pltpu.VMEM((2, BLK, HEAD), F32),
@@ -479,10 +500,10 @@
             pltpu.VMEM((4, piece, d), BF),
             pltpu.SemaphoreType.DMA((nsem,)),
             pltpu.SemaphoreType.DMA((nsem,)),
-            pltpu.SemaphoreType.DMA((5,)),
+            pltpu.SemaphoreType.DMA((12,)),
         ],
         compiler_params=pltpu.CompilerParams(
-            collective_id=0, has_side_effects=True, vmem_limit_bytes=60 * 1024 * 1024
+            collective_id=0, has_side_effects=True, vmem_limit_bytes=54 * 1024 * 1024
         ),
     )(
         sel_blocks, freqs, norm_gain.reshape(1, width), router_weight.reshape(1, width),

time: 70.7 us -> 69.7 us (0.986)
  no operation moved by 1% of the time
where the time goes in v6:
time: 69.7 us; the launch traced here: 69.4 us
  Pallas kernels  67.5 us (97%)
  local copies, waits for them, and re-layouts  1.87 us (3%)
    pallas_call x1, Pallas kernels, on_device(): pl.pallas_call(layer_kernel, name='layer', out_shape=jax.ShapeDtypeStruct...  67.5 us
    unnamed x1, local copies, waits for them, and re-layouts  1.87 us

profile of v6, /device:TPU:7, one launch (start us, length us, event | category | flops | bytes accessed | tf_op | source)
XLA Modules:
  0.0 69.4 jit_solution(3325937774471583382)
XLA Ops:
  0.0 67.5 %layer.1 = bf16[64,4096]{1,0:T(8,128)(2,1)} custom-call(s32[2]{0:T(128)} %sel.1, f32[1,128]{1,0:T(1,128)} %constant.2.clone.freq_hbm, f32[1,4096]{1,0:T(1,128)} %bitcast.4, f32[1,4096]{1,0:T(1,128)} %bitcast.5, bf16[16,128,1024]{2,1,0:T(8,128)(2,1)} %bitcast.3, bf16[4096,1024]{1,0:T(8,128)(2,1)} %wq_hbm.1, bf16[4096,128]{1,0:T(8,128)(2,1)} %wk_hbm.1, ...), custom_call_target="tpu_custom_call" | custom-call | tf_op jit(solution)/shard_map/layer/pallas_call | solution.py:457
  67.5 1.9 %copy.11 = bf16[64,4096]{1,0:T(8,128)(2,1)} copy(bf16[64,4096]{1,0:T(8,128)(2,1)} %layer.1) | data formatting | bytes 1048576

commit v7 on v6

--- a/solution.py
+++ b/solution.py
@@ -344,9 +344,9 @@
     for s in sides:
         s.half1[1].wait_recv()
         start(s.cross[2, 1])
-    attend([[(0, 0, 0), (0, 0, 1), (0, 2, 0), (0, 2, 1)]])
     relay(-1, 1)
     relay(1, 1)
+    attend([[(0, 0, 0), (0, 0, 1), (0, 2, 0), (0, 2, 1)]])
     last_groups = [
         [(di, dj, 1) for di in (-1, 1) for dj in (-1, 1)],
         [(di, 2, k) for di in (-1, 1) for k in range(2)],

time: 69.7 us -> 69.8 us (level)
  no operation moved by 1% of the time
where the time goes in v7:
time: 69.8 us; the launch traced here: 69.5 us
  Pallas kernels  67.6 us (97%)
  local copies, waits for them, and re-layouts  1.87 us (3%)
    pallas_call x1, Pallas kernels, on_device(): pl.pallas_call(layer_kernel, name='layer', out_shape=jax.ShapeDtypeStruct...  67.6 us
    unnamed x1, local copies, waits for them, and re-layouts  1.87 us

profile of v7, /device:TPU:7, one launch (start us, length us, event | category | flops | bytes accessed | tf_op | source)
XLA Modules:
  0.0 69.5 jit_solution(1721075821736661003)
XLA Ops:
  0.0 67.6 %layer.1 = bf16[64,4096]{1,0:T(8,128)(2,1)} custom-call(s32[2]{0:T(128)} %sel.1, f32[1,128]{1,0:T(1,128)} %constant.2.clone.freq_hbm, f32[1,4096]{1,0:T(1,128)} %bitcast.4, f32[1,4096]{1,0:T(1,128)} %bitcast.5, bf16[16,128,1024]{2,1,0:T(8,128)(2,1)} %bitcast.3, bf16[4096,1024]{1,0:T(8,128)(2,1)} %wq_hbm.1, bf16[4096,128]{1,0:T(8,128)(2,1)} %wk_hbm.1, ...), custom_call_target="tpu_custom_call" | custom-call | tf_op jit(solution)/shard_map/layer/pallas_call | solution.py:457
  67.6 1.9 %copy.11 = bf16[64,4096]{1,0:T(8,128)(2,1)} copy(bf16[64,4096]{1,0:T(8,128)(2,1)} %layer.1) | data formatting | bytes 1048576
